TPU v7x, 256 devices: a 8x8x2 block of a 8x8x16 slice. The times are simulated.
256 devices in a mesh: groups: 2 (over z), seq: 128 (over x, y, core).
Axes of the slice: x: 8, y: 8, z: 2, core: 2. Of those that a mesh axis runs over, the one named last changes fastest.
The devices are a block of a 8x8x16 slice.
Arguments:
- query_rows: bfloat16 [131072, 1536], P(('groups', 'seq')), parts along dimension 0, may hold values from -200 to 200
- key_rows: bfloat16 [131072, 1536], P(('groups', 'seq')), parts along dimension 0, may hold values from -6 to 6
- value_rows: bfloat16 [131072, 1536], P(('groups', 'seq')), parts along dimension 0, may hold values from -6 to 6
- select: int32 [512, 6], P('groups'), parts along dimension 0, may hold values from 0 to 255, as said below
- counts: int32 [512], P('groups'), parts along dimension 0, may hold values from 2 to 6, as said below
- guide_scale: float32 [2], P('groups'), parts along dimension 0, may hold values from 4 to 8
Outputs:
- guided: bfloat16 [65536, 1536], P(('groups', 'seq')), parts along dimension 0
There are 2 independent parts, one for each index of `groups`. A program takes and returns all parts, laid end to end along the dimension named above; each array names one. Nothing has to cross between parts.
Inputs may be any that keep to these rules, and one draw needn't show every extreme that they name: Row i begins with i itself. Its first counts[i] entries are distinct and name tiles of shards within 2 of tile i's shard, where tile t belongs to shard t // 4. The query tiles of one shard select at most 2 distinct tiles of any one other shard, and every shard selects 2 tiles of each shard within 2 in every draw. Entries past counts[i] are valid tile numbers that are not used. `counts`: whole shards are heavy or light, so the work of one device differs by about two times between devices.
All inputs are finite; a program needn't handle non-finite values.
Results may differ from a plain program's by a relative error of at most 0.0075.
Values may be sent and summed in bfloat16 or wider, within the bound.
No kernel may reach another device: no remote copies, remote signals or barrier semaphores. Data moves between devices by JAX's collectives and lax.ppermute only.
A program may use at most 128 MiB of HBM per device.

v0:
```python
import functools

import jax
import jax.numpy as jnp
from jax import lax
from jax.experimental import pallas as pl
from jax.experimental.pallas import tpu as pltpu
from jax.sharding import PartitionSpec as P

HEAD_DIM = 128
TILE = 128
REACH = 2
CAP = 2
OFFSETS = (1, 2, -1, -2)
CHUNKS = (5, 4, 2, 1)
EXP2_SCALE = HEAD_DIM ** (-0.5) * 1.4426950408889634
VMEM_BYTES = 24 << 20


SMEM = pl.BlockSpec(memory_space=pltpu.SMEM)
VMEM = pl.BlockSpec(memory_space=pltpu.VMEM)
HBM = pl.BlockSpec(memory_space=pltpu.HBM)
PARAMS = pltpu.CompilerParams(vmem_limit_bytes=VMEM_BYTES)


def shifted(block, axis, distance):
    devices = range(lax.axis_size(axis))
    route = [(i - distance, i) for i in devices if i - distance in devices]
    return lax.ppermute(block, axis, route)


def partner(block, axis):
    route = [(i, i ^ 1) for i in range(lax.axis_size(axis))]
    return lax.ppermute(block, axis, route)


def first_bit(bits):
    return jnp.where(
        bits & 1 != 0, 0, jnp.where(bits & 2 != 0, 1, jnp.where(bits & 4 != 0, 2, 3))
    )


def wanted_bits(select, counts, shard, tiles_dev, picks):
    bits = jnp.int32(0)
    base = (shard - REACH) * tiles_dev
    for row in range(tiles_dev):
        line = shard * tiles_dev + row
        live = counts[line]
        for pick in range(picks):
            place = jnp.clip(select[pick, line] - base, 0, (2 * REACH + 1) * tiles_dev - 1)
            bits = bits | jnp.where(pick < live, jnp.left_shift(1, place), 0)
    return bits


def fill_slots(my_shard, select, counts, table, tiles_dev, picks):
    bits = wanted_bits(select, counts, my_shard, tiles_dev, picks)
    for row in range(tiles_dev):
        line = my_shard * tiles_dev + row
        table[tiles_dev * picks + row] = counts[line]
        for pick in range(picks):
            tile = select[pick, line]
            away = jnp.clip(tile // tiles_dev - my_shard, -REACH, REACH)
            within = tile % tiles_dev
            theirs = jnp.right_shift(bits, (away + REACH) * tiles_dev)
            below = theirs & (jnp.left_shift(1, within) - 1)
            rank = (below & 1) + (jnp.right_shift(below, 1) & 1) + (jnp.right_shift(below, 2) & 1)
            rank = jnp.minimum(rank, CAP - 1)
            block = jnp.where(away < 0, -away - 1, away + REACH - 1)
            slot = jnp.where(away == 0, within, tiles_dev + block * CAP + rank)
            table[row * picks + pick] = slot


def pack_kernel(sizes, begins, widths, me, select, counts, keys, values, table, *rest):
    tiles_dev, picks, shards = sizes
    outs, (stage, sems) = rest[:-2], rest[-2:]
    loads = [
        pltpu.make_async_copy(keys, stage.at[0], sems.at[0]),
        pltpu.make_async_copy(values, stage.at[1], sems.at[1]),
    ]
    for load in loads:
        load.start()
    my_shard = me[0] // 2
    tiles = []
    for offset in OFFSETS:
        reader = jnp.clip(my_shard + offset, 0, shards - 1)
        bits = wanted_bits(select, counts, reader, tiles_dev, picks)
        mine = jnp.right_shift(bits, (REACH - offset) * tiles_dev) & 15
        tiles.append((first_bit(mine), first_bit(mine & (mine - 1))))
    fill_slots(my_shard, select, counts, table, tiles_dev, picks)
    for load in loads:
        load.wait()
    for index, (begin, width) in enumerate(zip(begins, widths)):
        for place in range(len(OFFSETS)):
            out = outs[index * len(OFFSETS) + place]
            for which in range(2):
                for slot in range(CAP):
                    rows = pl.ds(pl.multiple_of(tiles[place][slot] * TILE, TILE), TILE)
                    out[which, slot * TILE : (slot + 1) * TILE, :] = stage[
                        which, rows, begin : begin + width
                    ]


def attend_tile(queries, pool, result, slots, rows, begin, heads):
    for head in heads:
        cols = slice(head * HEAD_DIM, (head + 1) * HEAD_DIM)
        query = queries[rows, begin + head * HEAD_DIM : begin + (head + 1) * HEAD_DIM]
        keys = jnp.concatenate([pool[0, slot, cols] for slot in slots], axis=0)
        values = jnp.concatenate([pool[1, slot, cols] for slot in slots], axis=0)
        scores = lax.dot_general(
            query, keys, (((1,), (1,)), ((), ())), preferred_element_type=jnp.float32
        )
        top = jnp.max(scores, axis=1, keepdims=True)
        weights = jnp.exp2((scores - top) * EXP2_SCALE)
        total = jnp.sum(weights, axis=1, keepdims=True)
        mixed = jnp.dot(weights.astype(jnp.bfloat16), values, preferred_element_type=jnp.float32)
        result[rows, cols] = (mixed / total).astype(jnp.bfloat16)


def attend_kernel(begin, heads, picks, half, table, queries, keys, values, *rest):
    lands, (sent, kept, pool, result) = rest[:4], rest[4:]
    tokens = queries.shape[0]
    tiles_dev = tokens // TILE
    span = CAP * TILE
    width = heads * HEAD_DIM
    pool[0, :tokens, :] = keys[:, begin : begin + width]
    pool[1, :tokens, :] = values[:, begin : begin + width]
    for index, land in enumerate(lands):
        pool[:, tokens + index * span : tokens + (index + 1) * span, :] = land[...]

    def one_tile(tile, carry):
        rows = pl.ds(pl.multiple_of(tile * TILE, TILE), TILE)
        slots = [
            pl.ds(pl.multiple_of(table[tile * picks + pick] * TILE, TILE), TILE)
            for pick in range(picks)
        ]
        live = table[tiles_dev * picks + tile]
        for count in range(2, picks + 1):

            @pl.when(live == count)
            def _(count=count):
                attend_tile(queries, pool, result, slots[:count], rows, begin, range(heads))

        return carry

    lax.fori_loop(0, tiles_dev, one_tile, 0)
    half_rows = tokens // 2
    my_half = half[0]
    sent[...] = result[pl.ds(pl.multiple_of((1 - my_half) * half_rows, half_rows), half_rows), :]
    kept[...] = result[pl.ds(pl.multiple_of(my_half * half_rows, half_rows), half_rows), :]


def combine_kernel(begin, count, aliased, half, guide, *rest):
    pieces, rest = rest[: 2 * count], rest[2 * count + aliased :]
    out, mixed, sem = rest
    conditional = half[0] == 0
    guidance = guide[0]
    at = 0
    for index in range(count):
        own = pieces[index][...].astype(jnp.float32)
        theirs = pieces[count + index][...].astype(jnp.float32)
        cond = jnp.where(conditional, own, theirs)
        uncond = jnp.where(conditional, theirs, own)
        width = own.shape[1]
        mixed[:, at : at + width] = (uncond + guidance * (cond - uncond)).astype(jnp.bfloat16)
        at += width
    copy = pltpu.make_async_copy(mixed, out.at[:, pl.ds(begin, at)], sem)
    copy.start()
    copy.wait()


def body(query_rows, key_rows, value_rows, select, counts, guide_scale):
    shards = lax.axis_size("seq") // 2
    me = lax.axis_index("seq").astype(jnp.int32)
    my_half = (me % 2).reshape(1)
    tokens, row_width = query_rows.shape
    tiles_dev = tokens // TILE
    picks = select.shape[1]
    half_rows = tokens // 2
    dtype = query_rows.dtype
    span = CAP * TILE
    chunks = len(CHUNKS)
    begins = [sum(CHUNKS[:index]) * HEAD_DIM for index in range(chunks)]
    widths = [heads * HEAD_DIM for heads in CHUNKS]

    table, *packed = pl.pallas_call(
        functools.partial(pack_kernel, (tiles_dev, picks, shards), begins, widths),
        out_shape=[jax.ShapeDtypeStruct((tiles_dev * (picks + 1),), jnp.int32)]
        + [jax.ShapeDtypeStruct((2, span, width), dtype) for width in widths for _ in OFFSETS],
        in_specs=[SMEM, SMEM, SMEM, HBM, HBM],
        out_specs=[SMEM] + [VMEM] * (chunks * len(OFFSETS)),
        scratch_shapes=[pltpu.VMEM((2, tokens, row_width), dtype), pltpu.SemaphoreType.DMA((2,))],
        compiler_params=PARAMS,
        name="pack",
    )(me.reshape(1), select.T, counts, key_rows, value_rows)

    landed = []
    for index in range(chunks):
        boxes = packed[len(OFFSETS) * index : len(OFFSETS) * (index + 1)]
        landed.append([shifted(box, "seq", 2 * off) for box, off in zip(boxes, OFFSETS)])

    kept_all, their_all = [], []
    for index, (begin, width, heads) in enumerate(zip(begins, widths, CHUNKS)):
        sent, kept = pl.pallas_call(
            functools.partial(attend_kernel, begin, heads, picks),
            out_shape=[jax.ShapeDtypeStruct((half_rows, width), dtype)] * 2,
            in_specs=[SMEM, SMEM] + [VMEM] * 7,
            out_specs=[VMEM, VMEM],
            scratch_shapes=[
                pltpu.VMEM((2, tokens + len(OFFSETS) * span, width), dtype),
                pltpu.VMEM((tokens, width), dtype),
            ],
            compiler_params=PARAMS,
        )(my_half, table, query_rows, key_rows, value_rows, *landed[index])
        kept_all.append(kept)
        their_all.append(partner(sent, "seq"))

    early = chunks - 1
    guided = None
    for first, last in ((0, early), (early, chunks)):
        pieces = kept_all[first:last] + their_all[first:last]
        aliased = [] if guided is None else [guided]
        guided = pl.pallas_call(
            functools.partial(combine_kernel, begins[first], last - first, len(aliased)),
            out_shape=jax.ShapeDtypeStruct((half_rows, row_width), dtype),
            in_specs=[SMEM, SMEM] + [VMEM] * len(pieces) + [HBM] * len(aliased),
            out_specs=HBM,
            scratch_shapes=[
                pltpu.VMEM((half_rows, sum(widths[first:last])), dtype),
                pltpu.SemaphoreType.DMA,
            ],
            input_output_aliases={2 + len(pieces): 0} if aliased else {},
            compiler_params=PARAMS,
        )(my_half, guide_scale, *pieces, *aliased)
    return guided


def solution(mesh):
    in_specs = (
        P(("groups", "seq"), None),
        P(("groups", "seq"), None),
        P(("groups", "seq"), None),
        P("groups", None),
        P("groups"),
        P("groups"),
    )
    out_specs = P(("groups", "seq"), None)

    return jax.shard_map(body, mesh=mesh, in_specs=in_specs, out_specs=out_specs, check_vma=False)
```

profile of v0, /device:TPU:525, one launch (start us, length us, event | category | flops | bytes accessed | tf_op | source)
XLA Modules:
  0.0 187.1 jit_solution(4355249666518262677)
XLA Ops:
  4.2 3.2 %pack.1 = (s32[28]{0:T(128)S(1)}, bf16[2,256,640]{2,1,0:T(8,128)(2,1)S(1)}, bf16[2,256,640]{2,1,0:T(8,128)(2,1)S(1)}, bf16[2,256,640]{2,1,0:T(8,128)(2,1)S(1)}, ...) custom-call(s32[1]{0:T(128)} %bitcast.1.me, ...), custom_call_target="tpu_custom_call" | custom-call | tf_op jit(solution)/shard_map/pack/pallas_call | solution.py:185
  9.4 4.4 %collective-permute-start.9 = (bf16[2,256,512]{2,1,0:T(8,128)(2,1)S(1)}, bf16[2,256,512]{2,1,0:T(8,128)(2,1)S(1)}, u32[]{:S(2)}, u32[]{:S(2)}) collective-permute-start(bf16[2,256,512]{2,1,0:T(8,128)(2,1)S(1)} %get-tuple-element.42), channel_id=1, source_target_pairs={{0,2},{1,3},{2,4},{3,5},{4,6},{5,7},{6,8},{7,9},{8,10},{9,11},{10,... | collective-permute-start | bytes 1572872 | tf_op jit(solution)/shard_map/ppermute | solution.py:29
  13.8 6.6 %collective-permute-start.10 = (bf16[2,256,512]{2,1,0:T(8,128)(2,1)S(1)}, bf16[2,256,512]{2,1,0:T(8,128)(2,1)S(1)}, u32[]{:S(2)}, u32[]{:S(2)}) collective-permute-start(bf16[2,256,512]{2,1,0:T(8,128)(2,1)S(1)} %get-tuple-element.43), channel_id=1, source_target_pairs={{0,4},{1,5},{2,6},{3,7},{4,8},{5,9},{6,10},{7,11},{8,12},{9,13},{1... | collective-permute-start | bytes 1572872 | tf_op jit(solution)/shard_map/ppermute | solution.py:29
  20.5 7.1 %collective-permute-start.11 = (bf16[2,256,512]{2,1,0:T(8,128)(2,1)S(1)}, bf16[2,256,512]{2,1,0:T(8,128)(2,1)S(1)}, u32[]{:S(2)}, u32[]{:S(2)}) collective-permute-start(bf16[2,256,512]{2,1,0:T(8,128)(2,1)S(1)} %get-tuple-element.44), channel_id=1, source_target_pairs={{2,0},{3,1},{4,2},{5,3},{6,4},{7,5},{8,6},{9,7},{10,8},{11,9},{12,... | collective-permute-start | bytes 1572872 | tf_op jit(solution)/shard_map/ppermute | solution.py:29
  27.6 2.0 %collective-permute-start = (bf16[2,256,128]{2,1,0:T(8,128)(2,1)S(1)}, bf16[2,256,128]{2,1,0:T(8,128)(2,1)S(1)}, u32[]{:S(2)}, u32[]{:S(2)}) collective-permute-start(bf16[2,256,128]{2,1,0:T(8,128)(2,1)S(1)} %get-tuple-element.31), channel_id=1, source_target_pairs={{0,2},{1,3},{2,4},{3,5},{4,6},{5,7},{6,8},{7,9},{8,10},{9,11},{10,... | collective-permute-start | bytes 393224 | tf_op jit(solution)/shard_map/ppermute | solution.py:29
  29.5 2.1 %collective-permute-start.5 = (bf16[2,256,640]{2,1,0:T(8,128)(2,1)S(1)}, bf16[2,256,640]{2,1,0:T(8,128)(2,1)S(1)}, u32[]{:S(2)}, u32[]{:S(2)}) collective-permute-start(bf16[2,256,640]{2,1,0:T(8,128)(2,1)S(1)} %get-tuple-element.37), channel_id=1, source_target_pairs={{0,2},{1,3},{2,4},{3,5},{4,6},{5,7},{6,8},{7,9},{8,10},{9,11},{10,... | collective-permute-start | bytes 1966088 | tf_op jit(solution)/shard_map/ppermute | solution.py:29
  31.6 29.0 %collective-permute-done.rest_0_ = bf16[2,256,128]{2,1,0:T(8,128)(2,1)S(1)} collective-permute-done((bf16[2,256,128]{2,1,0:T(8,128)(2,1)S(1)}, bf16[2,256,128]{2,1,0:T(8,128)(2,1)S(1)}, u32[]{:S(2)}, u32[]{:S(2)}) %collective-permute-start) | collective-permute-done | bytes 131104 | tf_op jit(solution)/shard_map/ppermute | solution.py:29
  63.4 3.1 %collective-permute-start.7 = (bf16[2,256,640]{2,1,0:T(8,128)(2,1)S(1)}, bf16[2,256,640]{2,1,0:T(8,128)(2,1)S(1)}, u32[]{:S(2)}, u32[]{:S(2)}) collective-permute-start(bf16[2,256,640]{2,1,0:T(8,128)(2,1)S(1)} %get-tuple-element.39), channel_id=1, source_target_pairs={{2,0},{3,1},{4,2},{5,3},{6,4},{7,5},{8,6},{9,7},{10,8},{11,9},{12,... | collective-permute-start | bytes 1966088 | tf_op jit(solution)/shard_map/ppermute | solution.py:29
  67.3 5.2 %collective-permute-start.8 = (bf16[2,256,640]{2,1,0:T(8,128)(2,1)S(1)}, bf16[2,256,640]{2,1,0:T(8,128)(2,1)S(1)}, u32[]{:S(2)}, u32[]{:S(2)}) collective-permute-start(bf16[2,256,640]{2,1,0:T(8,128)(2,1)S(1)} %get-tuple-element.40), channel_id=1, source_target_pairs={{4,0},{5,1},{6,2},{7,3},{8,4},{9,5},{10,6},{11,7},{12,8},{13,9},{1... | collective-permute-start | bytes 1966088 | tf_op jit(solution)/shard_map/ppermute | solution.py:29
  73.3 1.9 %collective-permute-start.12 = (bf16[2,256,512]{2,1,0:T(8,128)(2,1)}, bf16[2,256,512]{2,1,0:T(8,128)(2,1)}, u32[]{:S(2)}, u32[]{:S(2)}) collective-permute-start(bf16[2,256,512]{2,1,0:T(8,128)(2,1)} %get-tuple-element.45), channel_id=1, source_target_pairs={{4,0},{5,1},{6,2},{7,3},{8,4},{9,5},{10,6},{11,7},{12,8},{13,9},{1... | collective-permute-start | bytes 1572872 | tf_op jit(solution)/shard_map/ppermute | solution.py:29
  75.3 6.8 %collective-permute-done.5.rest_0_ = bf16[2,256,640]{2,1,0:T(8,128)(2,1)S(1)} collective-permute-done((bf16[2,256,640]{2,1,0:T(8,128)(2,1)S(1)}, bf16[2,256,640]{2,1,0:T(8,128)(2,1)S(1)}, u32[]{:S(2)}, u32[]{:S(2)}) %collective-permute-start.5) | collective-permute-done | bytes 655392 | tf_op jit(solution)/shard_map/ppermute | solution.py:29
  84.9 4.7 %collective-permute-done.6.rest_1_ = bf16[2,256,640]{2,1,0:T(8,128)(2,1)S(1)} collective-permute-done((bf16[2,256,640]{2,1,0:T(8,128)(2,1)S(1)}, bf16[2,256,640]{2,1,0:T(8,128)(2,1)S(1)}, u32[]{:S(2)}, u32[]{:S(2)}) %collective-permute-start.6) | collective-permute-done | bytes 655392 | tf_op jit(solution)/shard_map/ppermute | solution.py:29
  92.4 2.9 %collective-permute-done.7.rest_2_ = bf16[2,256,640]{2,1,0:T(8,128)(2,1)S(1)} collective-permute-done((bf16[2,256,640]{2,1,0:T(8,128)(2,1)S(1)}, bf16[2,256,640]{2,1,0:T(8,128)(2,1)S(1)}, u32[]{:S(2)}, u32[]{:S(2)}) %collective-permute-start.7) | collective-permute-done | bytes 655392 | tf_op jit(solution)/shard_map/ppermute | solution.py:29
  96.1 19.5 %collective-permute-start.15 = (bf16[2,256,256]{2,1,0:T(8,128)(2,1)}, bf16[2,256,256]{2,1,0:T(8,128)(2,1)}, u32[]{:S(2)}, u32[]{:S(2)}) collective-permute-start(bf16[2,256,256]{2,1,0:T(8,128)(2,1)} %get-tuple-element.49), channel_id=1, source_target_pairs={{2,0},{3,1},{4,2},{5,3},{6,4},{7,5},{8,6},{9,7},{10,8},{11,9},{12,... | collective-permute-start | bytes 786440 | tf_op jit(solution)/shard_map/ppermute | solution.py:29
  116.4 5.2 %collective-permute-start.16 = (bf16[2,256,256]{2,1,0:T(8,128)(2,1)}, bf16[2,256,256]{2,1,0:T(8,128)(2,1)}, u32[]{:S(2)}, u32[]{:S(2)}) collective-permute-start(bf16[2,256,256]{2,1,0:T(8,128)(2,1)} %get-tuple-element.50), channel_id=1, source_target_pairs={{4,0},{5,1},{6,2},{7,3},{8,4},{9,5},{10,6},{11,7},{12,8},{13,9},{1... | collective-permute-start | bytes 786440 | tf_op jit(solution)/shard_map/ppermute | solution.py:29
  127.4 6.7 %shard_map.65 = (bf16[256,640]{1,0:T(8,128)(2,1)S(1)}, bf16[256,640]{1,0:T(8,128)(2,1)S(1)}) custom-call(s32[1]{0:T(128)} %bitcast.half, s32[28]{0:T(128)S(1)} %get-tuple-element.30.table, bf16[512,1536]{1,0:T(8,128)(2,1)S(1)} %copy-done.4, bf16[512,1536]{1,0:T(8,128)(2,1)S(1)} %copy-done.1, bf16[512,1536]{1,0:T(8,128)(2,1)S(1)} %copy-done.3, ...), custom_call_target="tpu_custom_call" | custom-call | tf_op jit(solution)/shard_map/pallas_call | solution.py:203
  135.7 19.4 %collective-permute-start.17 = (bf16[256,640]{1,0:T(8,128)(2,1)S(1)}, bf16[256,640]{1,0:T(8,128)(2,1)S(1)}, u32[]{:S(2)}, u32[]{:S(2)}) collective-permute-start(bf16[256,640]{1,0:T(8,128)(2,1)S(1)} %get-tuple-element.52), channel_id=1, source_target_pairs={{0,1},{1,0},{2,3},{3,2},{4,5},{5,4},{6,7},{7,6},{8,9},{9,8},{10,11... | collective-permute-start | bytes 983048 | tf_op jit(solution)/shard_map/ppermute | solution.py:34
  155.1 6.1 %shard_map.66 = (bf16[256,512]{1,0:T(8,128)(2,1)S(1)}, bf16[256,512]{1,0:T(8,128)(2,1)S(1)}) custom-call(s32[1]{0:T(128)} %bitcast.half, s32[28]{0:T(128)S(1)} %get-tuple-element.30.table, bf16[512,1536]{1,0:T(8,128)(2,1)S(1)} %copy-done.4, bf16[512,1536]{1,0:T(8,128)(2,1)S(1)} %copy-done.1, bf16[512,1536]{1,0:T(8,128)(2,1)S(1)} %copy-done.3, ...), custom_call_target="tpu_custom_call" | custom-call | tf_op jit(solution)/shard_map/pallas_call | solution.py:203
  161.2 4.6 %collective-permute-start.1 = (bf16[2,256,128]{2,1,0:T(8,128)(2,1)S(1)}, bf16[2,256,128]{2,1,0:T(8,128)(2,1)S(1)}, u32[]{:S(2)}, u32[]{:S(2)}) collective-permute-start(bf16[2,256,128]{2,1,0:T(8,128)(2,1)S(1)} %copy-done.26), channel_id=1, source_target_pairs={{0,4},{1,5},{2,6},{3,7},{4,8},{5,9},{6,10},{7,11},{8,12},{9,13},{1... | collective-permute-start | bytes 393224 | tf_op jit(solution)/shard_map/ppermute | solution.py:29
  166.3 4.3 %collective-permute-start.2 = (bf16[2,256,128]{2,1,0:T(8,128)(2,1)S(1)}, bf16[2,256,128]{2,1,0:T(8,128)(2,1)S(1)}, u32[]{:S(2)}, u32[]{:S(2)}) collective-permute-start(bf16[2,256,128]{2,1,0:T(8,128)(2,1)S(1)} %copy-done.24), channel_id=1, source_target_pairs={{2,0},{3,1},{4,2},{5,3},{6,4},{7,5},{8,6},{9,7},{10,8},{11,9},{12,... | collective-permute-start | bytes 393224 | tf_op jit(solution)/shard_map/ppermute | solution.py:29
  170.6 2.0 %collective-permute-start.3 = (bf16[2,256,128]{2,1,0:T(8,128)(2,1)S(1)}, bf16[2,256,128]{2,1,0:T(8,128)(2,1)S(1)}, u32[]{:S(2)}, u32[]{:S(2)}) collective-permute-start(bf16[2,256,128]{2,1,0:T(8,128)(2,1)S(1)} %copy-done.22), channel_id=1, source_target_pairs={{4,0},{5,1},{6,2},{7,3},{8,4},{9,5},{10,6},{11,7},{12,8},{13,9},{1... | collective-permute-start | bytes 393224 | tf_op jit(solution)/shard_map/ppermute | solution.py:29
  172.6 4.0 %shard_map.67 = (bf16[256,256]{1,0:T(8,128)(2,1)S(1)}, bf16[256,256]{1,0:T(8,128)(2,1)S(1)}) custom-call(s32[1]{0:T(128)} %bitcast.half, s32[28]{0:T(128)S(1)} %get-tuple-element.30.table, bf16[512,1536]{1,0:T(8,128)(2,1)S(1)} %copy-done.4, bf16[512,1536]{1,0:T(8,128)(2,1)S(1)} %copy-done.1, bf16[512,1536]{1,0:T(8,128)(2,1)S(1)} %copy-done.3, ...), custom_call_target="tpu_custom_call" | custom-call | tf_op jit(solution)/shard_map/pallas_call | solution.py:203
  177.2 3.9 %collective-permute-done.3.rest_3_ = bf16[2,256,128]{2,1,0:T(8,128)(2,1)S(1)} collective-permute-done((bf16[2,256,128]{2,1,0:T(8,128)(2,1)S(1)}, bf16[2,256,128]{2,1,0:T(8,128)(2,1)S(1)}, u32[]{:S(2)}, u32[]{:S(2)}) %collective-permute-start.3) | collective-permute-done | bytes 131104 | tf_op jit(solution)/shard_map/ppermute | solution.py:29
  181.0 2.4 %shard_map.64 = (bf16[256,128]{1,0:T(8,128)(2,1)S(1)}, bf16[256,128]{1,0:T(8,128)(2,1)S(1)}) custom-call(s32[1]{0:T(128)} %bitcast.half, s32[28]{0:T(128)S(1)} %get-tuple-element.30.table, bf16[512,1536]{1,0:T(8,128)(2,1)S(1)} %copy-done.4, bf16[512,1536]{1,0:T(8,128)(2,1)S(1)} %copy-done.1, bf16[512,1536]{1,0:T(8,128)(2,1)S(1)} %copy-done.3, ...), custom_call_target="tpu_custom_call" | custom-call | tf_op jit(solution)/shard_map/pallas_call | solution.py:203
  (77 shorter events, 28.9 us)
Async XLA Ops:
  4.2 117.4 %copy-start.1 = (bf16[512,1536]{1,0:T(8,128)(2,1)S(1)}, bf16[512,1536]{1,0:T(8,128)(2,1)}, u32[]{:S(2)}) copy-start(bf16[512,1536]{1,0:T(8,128)(2,1)} %keys.9) | copy-start | bytes 4718596
  4.2 117.4 %copy-start.3 = (bf16[512,1536]{1,0:T(8,128)(2,1)S(1)}, bf16[512,1536]{1,0:T(8,128)(2,1)}, u32[]{:S(2)}) copy-start(bf16[512,1536]{1,0:T(8,128)(2,1)} %values.9) | copy-start | bytes 4718596
  9.4 53.2 %collective-permute-start.9 = (bf16[2,256,512]{2,1,0:T(8,128)(2,1)S(1)}, bf16[2,256,512]{2,1,0:T(8,128)(2,1)S(1)}, u32[]{:S(2)}, u32[]{:S(2)}) collective-permute-start(bf16[2,256,512]{2,1,0:T(8,128)(2,1)S(1)} %get-tuple-element.42), channel_id=1, source_target_pairs={{0,2},{1,3},{2,4},{3,5},{4,6},{5,7},{6,8},{7,9},{8,10},{9,11},{10,... | collective-permute-start | bytes 1572872 | tf_op jit(solution)/shard_map/ppermute | solution.py:29
  13.8 52.7 %collective-permute-start.10 = (bf16[2,256,512]{2,1,0:T(8,128)(2,1)S(1)}, bf16[2,256,512]{2,1,0:T(8,128)(2,1)S(1)}, u32[]{:S(2)}, u32[]{:S(2)}) collective-permute-start(bf16[2,256,512]{2,1,0:T(8,128)(2,1)S(1)} %get-tuple-element.43), channel_id=1, source_target_pairs={{0,4},{1,5},{2,6},{3,7},{4,8},{5,9},{6,10},{7,11},{8,12},{9,13},{1... | collective-permute-start | bytes 1572872 | tf_op jit(solution)/shard_map/ppermute | solution.py:29
  20.5 52.1 %collective-permute-start.11 = (bf16[2,256,512]{2,1,0:T(8,128)(2,1)S(1)}, bf16[2,256,512]{2,1,0:T(8,128)(2,1)S(1)}, u32[]{:S(2)}, u32[]{:S(2)}) collective-permute-start(bf16[2,256,512]{2,1,0:T(8,128)(2,1)S(1)} %get-tuple-element.44), channel_id=1, source_target_pairs={{2,0},{3,1},{4,2},{5,3},{6,4},{7,5},{8,6},{9,7},{10,8},{11,9},{12,... | collective-permute-start | bytes 1572872 | tf_op jit(solution)/shard_map/ppermute | solution.py:29
  27.6 33.0 %collective-permute-start = (bf16[2,256,128]{2,1,0:T(8,128)(2,1)S(1)}, bf16[2,256,128]{2,1,0:T(8,128)(2,1)S(1)}, u32[]{:S(2)}, u32[]{:S(2)}) collective-permute-start(bf16[2,256,128]{2,1,0:T(8,128)(2,1)S(1)} %get-tuple-element.31), channel_id=1, source_target_pairs={{0,2},{1,3},{2,4},{3,5},{4,6},{5,7},{6,8},{7,9},{8,10},{9,11},{10,... | collective-permute-start | bytes 393224 | tf_op jit(solution)/shard_map/ppermute | solution.py:29
  29.5 52.6 %collective-permute-start.5 = (bf16[2,256,640]{2,1,0:T(8,128)(2,1)S(1)}, bf16[2,256,640]{2,1,0:T(8,128)(2,1)S(1)}, u32[]{:S(2)}, u32[]{:S(2)}) collective-permute-start(bf16[2,256,640]{2,1,0:T(8,128)(2,1)S(1)} %get-tuple-element.37), channel_id=1, source_target_pairs={{0,2},{1,3},{2,4},{3,5},{4,6},{5,7},{6,8},{7,9},{8,10},{9,11},{10,... | collective-permute-start | bytes 1966088 | tf_op jit(solution)/shard_map/ppermute | solution.py:29
  60.6 29.0 %collective-permute-start.6 = (bf16[2,256,640]{2,1,0:T(8,128)(2,1)S(1)}, bf16[2,256,640]{2,1,0:T(8,128)(2,1)S(1)}, u32[]{:S(2)}, u32[]{:S(2)}) collective-permute-start(bf16[2,256,640]{2,1,0:T(8,128)(2,1)S(1)} %get-tuple-element.38), channel_id=1, source_target_pairs={{0,4},{1,5},{2,6},{3,7},{4,8},{5,9},{6,10},{7,11},{8,12},{9,13},{1... | collective-permute-start | bytes 1966088 | tf_op jit(solution)/shard_map/ppermute | solution.py:29
  63.4 31.9 %collective-permute-start.7 = (bf16[2,256,640]{2,1,0:T(8,128)(2,1)S(1)}, bf16[2,256,640]{2,1,0:T(8,128)(2,1)S(1)}, u32[]{:S(2)}, u32[]{:S(2)}) collective-permute-start(bf16[2,256,640]{2,1,0:T(8,128)(2,1)S(1)} %get-tuple-element.39), channel_id=1, source_target_pairs={{2,0},{3,1},{4,2},{5,3},{6,4},{7,5},{8,6},{9,7},{10,8},{11,9},{12,... | collective-permute-start | bytes 1966088 | tf_op jit(solution)/shard_map/ppermute | solution.py:29
  67.3 48.3 %collective-permute-start.8 = (bf16[2,256,640]{2,1,0:T(8,128)(2,1)S(1)}, bf16[2,256,640]{2,1,0:T(8,128)(2,1)S(1)}, u32[]{:S(2)}, u32[]{:S(2)}) collective-permute-start(bf16[2,256,640]{2,1,0:T(8,128)(2,1)S(1)} %get-tuple-element.40), channel_id=1, source_target_pairs={{4,0},{5,1},{6,2},{7,3},{8,4},{9,5},{10,6},{11,7},{12,8},{13,9},{1... | collective-permute-start | bytes 1966088 | tf_op jit(solution)/shard_map/ppermute | solution.py:29
  73.3 62.3 %collective-permute-start.12 = (bf16[2,256,512]{2,1,0:T(8,128)(2,1)}, bf16[2,256,512]{2,1,0:T(8,128)(2,1)}, u32[]{:S(2)}, u32[]{:S(2)}) collective-permute-start(bf16[2,256,512]{2,1,0:T(8,128)(2,1)} %get-tuple-element.45), channel_id=1, source_target_pairs={{4,0},{5,1},{6,2},{7,3},{8,4},{9,5},{10,6},{11,7},{12,8},{13,9},{1... | collective-permute-start | bytes 1572872 | tf_op jit(solution)/shard_map/ppermute | solution.py:29
  82.9 78.3 %collective-permute-start.13 = (bf16[2,256,256]{2,1,0:T(8,128)(2,1)}, bf16[2,256,256]{2,1,0:T(8,128)(2,1)S(1)}, u32[]{:S(2)}, u32[]{:S(2)}) collective-permute-start(bf16[2,256,256]{2,1,0:T(8,128)(2,1)} %get-tuple-element.47), channel_id=1, source_target_pairs={{0,2},{1,3},{2,4},{3,5},{4,6},{5,7},{6,8},{7,9},{8,10},{9,11},{10,... | collective-permute-start | bytes 786440 | tf_op jit(solution)/shard_map/ppermute | solution.py:29
  90.4 75.4 %collective-permute-start.14 = (bf16[2,256,256]{2,1,0:T(8,128)(2,1)}, bf16[2,256,256]{2,1,0:T(8,128)(2,1)}, u32[]{:S(2)}, u32[]{:S(2)}) collective-permute-start(bf16[2,256,256]{2,1,0:T(8,128)(2,1)} %get-tuple-element.48), channel_id=1, source_target_pairs={{0,4},{1,5},{2,6},{3,7},{4,8},{5,9},{6,10},{7,11},{8,12},{9,13},{1... | collective-permute-start | bytes 786440 | tf_op jit(solution)/shard_map/ppermute | solution.py:29
  96.1 70.2 %collective-permute-start.15 = (bf16[2,256,256]{2,1,0:T(8,128)(2,1)}, bf16[2,256,256]{2,1,0:T(8,128)(2,1)}, u32[]{:S(2)}, u32[]{:S(2)}) collective-permute-start(bf16[2,256,256]{2,1,0:T(8,128)(2,1)} %get-tuple-element.49), channel_id=1, source_target_pairs={{2,0},{3,1},{4,2},{5,3},{6,4},{7,5},{8,6},{9,7},{10,8},{11,9},{12,... | collective-permute-start | bytes 786440 | tf_op jit(solution)/shard_map/ppermute | solution.py:29
  116.4 54.2 %collective-permute-start.16 = (bf16[2,256,256]{2,1,0:T(8,128)(2,1)}, bf16[2,256,256]{2,1,0:T(8,128)(2,1)}, u32[]{:S(2)}, u32[]{:S(2)}) collective-permute-start(bf16[2,256,256]{2,1,0:T(8,128)(2,1)} %get-tuple-element.50), channel_id=1, source_target_pairs={{4,0},{5,1},{6,2},{7,3},{8,4},{9,5},{10,6},{11,7},{12,8},{13,9},{1... | collective-permute-start | bytes 786440 | tf_op jit(solution)/shard_map/ppermute | solution.py:29
  135.7 30.6 %copy-start.24 = (bf16[2,256,128]{2,1,0:T(8,128)(2,1)S(1)}, bf16[2,256,128]{2,1,0:T(8,128)(2,1)}, u32[]{:S(2)}) copy-start(bf16[2,256,128]{2,1,0:T(8,128)(2,1)} %copy-done.23) | copy-start | bytes 393220
  135.7 34.9 %copy-start.22 = (bf16[2,256,128]{2,1,0:T(8,128)(2,1)S(1)}, bf16[2,256,128]{2,1,0:T(8,128)(2,1)}, u32[]{:S(2)}) copy-start(bf16[2,256,128]{2,1,0:T(8,128)(2,1)} %copy-done.21) | copy-start | bytes 393220
  135.7 49.3 %collective-permute-start.17 = (bf16[256,640]{1,0:T(8,128)(2,1)S(1)}, bf16[256,640]{1,0:T(8,128)(2,1)S(1)}, u32[]{:S(2)}, u32[]{:S(2)}) collective-permute-start(bf16[256,640]{1,0:T(8,128)(2,1)S(1)} %get-tuple-element.52), channel_id=1, source_target_pairs={{0,1},{1,0},{2,3},{3,2},{4,5},{5,4},{6,7},{7,6},{8,9},{9,8},{10,11... | collective-permute-start | bytes 983048 | tf_op jit(solution)/shard_map/ppermute | solution.py:34
  161.2 15.4 %collective-permute-start.1 = (bf16[2,256,128]{2,1,0:T(8,128)(2,1)S(1)}, bf16[2,256,128]{2,1,0:T(8,128)(2,1)S(1)}, u32[]{:S(2)}, u32[]{:S(2)}) collective-permute-start(bf16[2,256,128]{2,1,0:T(8,128)(2,1)S(1)} %copy-done.26), channel_id=1, source_target_pairs={{0,4},{1,5},{2,6},{3,7},{4,8},{5,9},{6,10},{7,11},{8,12},{9,13},{1... | collective-permute-start | bytes 393224 | tf_op jit(solution)/shard_map/ppermute | solution.py:29
  165.8 19.2 %collective-permute-start.18 = (bf16[256,512]{1,0:T(8,128)(2,1)S(1)}, bf16[256,512]{1,0:T(8,128)(2,1)S(1)}, u32[]{:S(2)}, u32[]{:S(2)}) collective-permute-start(bf16[256,512]{1,0:T(8,128)(2,1)S(1)} %get-tuple-element.53), channel_id=1, source_target_pairs={{0,1},{1,0},{2,3},{3,2},{4,5},{5,4},{6,7},{7,6},{8,9},{9,8},{10,11... | collective-permute-start | bytes 786440 | tf_op jit(solution)/shard_map/ppermute | solution.py:34
  166.3 10.9 %collective-permute-start.2 = (bf16[2,256,128]{2,1,0:T(8,128)(2,1)S(1)}, bf16[2,256,128]{2,1,0:T(8,128)(2,1)S(1)}, u32[]{:S(2)}, u32[]{:S(2)}) collective-permute-start(bf16[2,256,128]{2,1,0:T(8,128)(2,1)S(1)} %copy-done.24), channel_id=1, source_target_pairs={{2,0},{3,1},{4,2},{5,3},{6,4},{7,5},{8,6},{9,7},{10,8},{11,9},{12,... | collective-permute-start | bytes 393224 | tf_op jit(solution)/shard_map/ppermute | solution.py:29
  170.6 10.4 %collective-permute-start.3 = (bf16[2,256,128]{2,1,0:T(8,128)(2,1)S(1)}, bf16[2,256,128]{2,1,0:T(8,128)(2,1)S(1)}, u32[]{:S(2)}, u32[]{:S(2)}) collective-permute-start(bf16[2,256,128]{2,1,0:T(8,128)(2,1)S(1)} %copy-done.22), channel_id=1, source_target_pairs={{4,0},{5,1},{6,2},{7,3},{8,4},{9,5},{10,6},{11,7},{12,8},{13,9},{1... | collective-permute-start | bytes 393224 | tf_op jit(solution)/shard_map/ppermute | solution.py:29
  176.6 8.4 %collective-permute-start.19 = (bf16[256,256]{1,0:T(8,128)(2,1)S(1)}, bf16[256,256]{1,0:T(8,128)(2,1)S(1)}, u32[]{:S(2)}, u32[]{:S(2)}) collective-permute-start(bf16[256,256]{1,0:T(8,128)(2,1)S(1)} %get-tuple-element.54), channel_id=1, source_target_pairs={{0,1},{1,0},{2,3},{3,2},{4,5},{5,4},{6,7},{7,6},{8,9},{9,8},{10,11... | collective-permute-start | bytes 393224 | tf_op jit(solution)/shard_map/ppermute | solution.py:34
  183.4 2.8 %collective-permute-start.4 = (bf16[256,128]{1,0:T(8,128)(2,1)S(1)}, bf16[256,128]{1,0:T(8,128)(2,1)S(1)}, u32[]{:S(2)}, u32[]{:S(2)}) collective-permute-start(bf16[256,128]{1,0:T(8,128)(2,1)S(1)} %get-tuple-element.36), channel_id=1, source_target_pairs={{0,1},{1,0},{2,3},{3,2},{4,5},{5,4},{6,7},{7,6},{8,9},{9,8},{10,11... | collective-permute-start | bytes 196616 | tf_op jit(solution)/shard_map/ppermute | solution.py:34
  (23 other events, 126.3 us)
where the time goes:
time: 188 us; the launch traced here: 187 us
  starting transfers between devices  95.2 us (51%)
  waiting for transfers between devices  48.8 us (26%)
  Pallas kernels  24.3 us (13%)
  local copies, waits for them, and re-layouts  17.7 us (9%)
    ppermute x16, starting transfers between devices, shifted(): return lax.ppermute(block, axis, route)  73.8 us
    ppermute x16, waiting for transfers between devices, shifted(): return lax.ppermute(block, axis, route)  48.8 us
    ppermute x4, starting transfers between devices, partner(): return lax.ppermute(block, axis, route)  21.4 us
    pallas_call x4, Pallas kernels, body(): pl.pallas_call(functools.partial(attend_kernel, begin, heads, picks), out...  19.2 us
    unnamed x54, local copies, waits for them, and re-layouts  17.7 us
  transfers between devices with their start and end apart: 20, of which 6 were waited for; matrix products, arithmetic and copies ran while one was open for 0% of the time, Pallas kernels for 11%

commit v1 on v0

--- a/solution.py
+++ b/solution.py
@@ -11,8 +11,9 @@
 TILE = 128
 REACH = 2
 CAP = 2
-OFFSETS = (1, 2, -1, -2)
-CHUNKS = (5, 4, 2, 1)
+OFFSETS = (1, -1, 2, -2)
+NEAR = 2
+CHUNKS = (6, 5, 1)
 EXP2_SCALE = HEAD_DIM ** (-0.5) * 1.4426950408889634
 VMEM_BYTES = 24 << 20
 
@@ -52,7 +53,7 @@
     return bits
 
 
-def fill_slots(my_shard, select, counts, table, tiles_dev, picks):
+def fill_table(my_shard, tiles, select, counts, table, tiles_dev, picks):
     bits = wanted_bits(select, counts, my_shard, tiles_dev, picks)
     for row in range(tiles_dev):
         line = my_shard * tiles_dev + row
@@ -65,38 +66,70 @@
             below = theirs & (jnp.left_shift(1, within) - 1)
             rank = (below & 1) + (jnp.right_shift(below, 1) & 1) + (jnp.right_shift(below, 2) & 1)
             rank = jnp.minimum(rank, CAP - 1)
-            block = jnp.where(away < 0, -away - 1, away + REACH - 1)
+            block = 2 * (jnp.abs(away) - 1) + jnp.where(away < 0, 0, 1)
             slot = jnp.where(away == 0, within, tiles_dev + block * CAP + rank)
             table[row * picks + pick] = slot
-
-
-def pack_kernel(sizes, begins, widths, me, select, counts, keys, values, table, *rest):
-    tiles_dev, picks, shards = sizes
-    outs, (stage, sems) = rest[:-2], rest[-2:]
-    loads = [
-        pltpu.make_async_copy(keys, stage.at[0], sems.at[0]),
-        pltpu.make_async_copy(values, stage.at[1], sems.at[1]),
-    ]
+    for index, tile in enumerate(tiles):
+        table[tiles_dev * (picks + 1) + index] = tile
+
+
+def sent_tiles(my_shard, offset, select, counts, tiles_dev, picks, shards):
+    reader = jnp.clip(my_shard + offset, 0, shards - 1)
+    bits = wanted_bits(select, counts, reader, tiles_dev, picks)
+    mine = jnp.right_shift(bits, (REACH - offset) * tiles_dev) & 15
+    return [first_bit(mine), first_bit(mine & (mine - 1))]
+
+
+def tile_rows(tile):
+    return pl.ds(pl.multiple_of(tile * TILE, TILE), TILE)
+
+
+def pack_near_kernel(sizes, me, select, counts, keys, values, table, *rest):
+    outs, (stage, load_sems, sems) = rest[:NEAR], rest[NEAR:]
+    my_shard = me[0] // 2
+    loads = []
+    for which, rows in enumerate((keys, values)):
+        for tile in range(sizes[0]):
+            part = pl.ds(tile * TILE, TILE)
+            loads.append(
+                pltpu.make_async_copy(
+                    rows.at[part, :], stage.at[which, part, :], load_sems.at[len(loads)]
+                )
+            )
     for load in loads:
         load.start()
-    my_shard = me[0] // 2
-    tiles = []
-    for offset in OFFSETS:
-        reader = jnp.clip(my_shard + offset, 0, shards - 1)
-        bits = wanted_bits(select, counts, reader, tiles_dev, picks)
-        mine = jnp.right_shift(bits, (REACH - offset) * tiles_dev) & 15
-        tiles.append((first_bit(mine), first_bit(mine & (mine - 1))))
-    fill_slots(my_shard, select, counts, table, tiles_dev, picks)
+    near = [sent_tiles(my_shard, off, select, counts, *sizes) for off in OFFSETS[:NEAR]]
     for load in loads:
         load.wait()
+    copies = []
+    for index, chosen in enumerate(near):
+        for slot, tile in enumerate(chosen):
+            for which in range(2):
+                copy = pltpu.make_async_copy(
+                    stage.at[which, tile_rows(tile), :],
+                    outs[index].at[which, pl.ds(slot * TILE, TILE), :],
+                    sems.at[len(copies)],
+                )
+                copy.start()
+                copies.append(copy)
+    tiles = []
+    for offset in OFFSETS[NEAR:]:
+        tiles += sent_tiles(my_shard, offset, select, counts, *sizes)
+    fill_table(my_shard, tiles, select, counts, table, *sizes[:2])
+    for copy in copies:
+        copy.wait()
+
+
+def pack_far_kernel(first, begins, widths, table, keys, values, *outs):
+    far = len(OFFSETS) - NEAR
     for index, (begin, width) in enumerate(zip(begins, widths)):
-        for place in range(len(OFFSETS)):
-            out = outs[index * len(OFFSETS) + place]
-            for which in range(2):
-                for slot in range(CAP):
-                    rows = pl.ds(pl.multiple_of(tiles[place][slot] * TILE, TILE), TILE)
-                    out[which, slot * TILE : (slot + 1) * TILE, :] = stage[
-                        which, rows, begin : begin + width
+        for place in range(far):
+            out = outs[index * far + place]
+            for slot in range(CAP):
+                rows = tile_rows(table[first + place * CAP + slot])
+                for which, source in enumerate((keys, values)):
+                    out[which, slot * TILE : (slot + 1) * TILE, :] = source[
+                        rows, begin : begin + width
                     ]
 
 
@@ -125,7 +158,10 @@
     pool[0, :tokens, :] = keys[:, begin : begin + width]
     pool[1, :tokens, :] = values[:, begin : begin + width]
     for index, land in enumerate(lands):
-        pool[:, tokens + index * span : tokens + (index + 1) * span, :] = land[...]
+        at = begin if index < NEAR else 0
+        pool[:, tokens + index * span : tokens + (index + 1) * span, :] = land[
+            :, :, at : at + width
+        ]
 
     def one_tile(tile, carry):
         rows = pl.ds(pl.multiple_of(tile * TILE, TILE), TILE)
@@ -182,21 +218,41 @@
     begins = [sum(CHUNKS[:index]) * HEAD_DIM for index in range(chunks)]
     widths = [heads * HEAD_DIM for heads in CHUNKS]
 
+    far = len(OFFSETS) - NEAR
+
+    def box(width):
+        return jax.ShapeDtypeStruct((2, span, width), dtype)
+
+    table_size = tiles_dev * (picks + 1) + far * CAP
     table, *packed = pl.pallas_call(
-        functools.partial(pack_kernel, (tiles_dev, picks, shards), begins, widths),
-        out_shape=[jax.ShapeDtypeStruct((tiles_dev * (picks + 1),), jnp.int32)]
-        + [jax.ShapeDtypeStruct((2, span, width), dtype) for width in widths for _ in OFFSETS],
+        functools.partial(pack_near_kernel, (tiles_dev, picks, shards)),
+        out_shape=[jax.ShapeDtypeStruct((table_size,), jnp.int32)] + [box(row_width)] * NEAR,
         in_specs=[SMEM, SMEM, SMEM, HBM, HBM],
-        out_specs=[SMEM] + [VMEM] * (chunks * len(OFFSETS)),
-        scratch_shapes=[pltpu.VMEM((2, tokens, row_width), dtype), pltpu.SemaphoreType.DMA((2,))],
+        out_specs=[SMEM] + [HBM] * NEAR,
+        scratch_shapes=[
+            pltpu.VMEM((2, tokens, row_width), dtype),
+            pltpu.SemaphoreType.DMA((2 * tiles_dev,)),
+            pltpu.SemaphoreType.DMA((NEAR * CAP * 2,)),
+        ],
+        name="pack_near",
+    )(me.reshape(1), select.T, counts, key_rows, value_rows)
+    near = [shifted(piece, "seq", 2 * off) for piece, off in zip(packed, OFFSETS)]
+    packed = pl.pallas_call(
+        functools.partial(pack_far_kernel, tiles_dev * (picks + 1), begins, widths),
+        out_shape=[box(width) for width in widths for _ in range(far)],
+        in_specs=[SMEM, VMEM, VMEM],
+        out_specs=[VMEM] * (chunks * far),
         compiler_params=PARAMS,
-        name="pack",
-    )(me.reshape(1), select.T, counts, key_rows, value_rows)
+        name="pack_far",
+    )(table, key_rows, value_rows)
 
     landed = []
     for index in range(chunks):
-        boxes = packed[len(OFFSETS) * index : len(OFFSETS) * (index + 1)]
-        landed.append([shifted(box, "seq", 2 * off) for box, off in zip(boxes, OFFSETS)])
+        pieces = packed[far * index : far * (index + 1)]
+        landed.append(
+            near
+            + [shifted(piece, "seq", 2 * off) for piece, off in zip(pieces, OFFSETS[NEAR:])]
+        )
 
     kept_all, their_all = [], []
     for index, (begin, width, heads) in enumerate(zip(begins, widths, CHUNKS)):

time: 188 us -> 156 us (0.83)
  the two profiles are of different devices: /device:TPU:525 before, /device:TPU:647 now
where the time goes in v1:
time: 156 us
  starting transfers between devices  73.9 us (47%)
  waiting for transfers between devices  44.1 us (28%)
  Pallas kernels  32.7 us (21%)
  local copies, waits for them, and re-layouts  4.08 us (3%)
    ppermute x8, starting transfers between devices, shifted(): return lax.ppermute(block, axis, route)  68.3 us
    ppermute x8, waiting for transfers between devices, shifted(): return lax.ppermute(block, axis, route)  44.1 us
    pallas_call x3, Pallas kernels, body(): pl.pallas_call(functools.partial(attend_kernel, begin, heads, picks), out...  23.6 us
    ppermute x3, starting transfers between devices, partner(): return lax.ppermute(block, axis, route)  5.64 us
    pallas_call x1, Pallas kernels, body(): pl.pallas_call(functools.partial(pack_near_kernel, (tiles_dev, picks, sha...  5.11 us
    unnamed x14, local copies, waits for them, and re-layouts  4.08 us
  transfers between devices with their start and end apart: 11, of which 4 were waited for; matrix products, arithmetic and copies ran while one was open for 0% of the time, Pallas kernels for 17%

profile of v1, /device:TPU:647, one launch (start us, length us, event | category | flops | bytes accessed | tf_op | source)
XLA Modules:
  0.0 155.8 jit_solution(4560728872325437334)
XLA Ops:
  0.0 5.1 %pack_near.1 = (s32[32]{0:T(128)}, bf16[2,256,1536]{2,1,0:T(8,128)(2,1)}, bf16[2,256,1536]{2,1,0:T(8,128)(2,1)}) custom-call(s32[1]{0:T(128)} %bitcast.1.me, s32[6,256]{1,0:T(8,128)} %bitcast.3, s32[256]{0:T(256)} %counts.1, bf16[512,1536]{1,0:T(8,128)(2,1)} %keys.9, bf16[512,1536]{1,0:T(8,128)(2,1)} %values.9), custom_call_target="tpu_custom_call" | custom-call | tf_op jit(solution)/shard_map/pack_near/pallas_call | solution.py:227
  5.1 4.4 %collective-permute-start = (bf16[2,256,1536]{2,1,0:T(8,128)(2,1)}, bf16[2,256,1536]{2,1,0:T(8,128)(2,1)}, u32[]{:S(2)}, u32[]{:S(2)}) collective-permute-start(bf16[2,256,1536]{2,1,0:T(8,128)(2,1)} %get-tuple-element.21), channel_id=1, source_target_pairs={{0,2},{1,3},{2,4},{3,5},{4,6},{5,7},{6,8},{7,9},{8,10},{9,11},{10,... | collective-permute-start | bytes 4718600 | tf_op jit(solution)/shard_map/ppermute | solution.py:30
  9.6 10.9 %collective-permute-start.1 = (bf16[2,256,1536]{2,1,0:T(8,128)(2,1)}, bf16[2,256,1536]{2,1,0:T(8,128)(2,1)}, u32[]{:S(2)}, u32[]{:S(2)}) collective-permute-start(bf16[2,256,1536]{2,1,0:T(8,128)(2,1)} %get-tuple-element.22), channel_id=1, source_target_pairs={{2,0},{3,1},{4,2},{5,3},{6,4},{7,5},{8,6},{9,7},{10,8},{11,9},{12,... | collective-permute-start | bytes 4718600 | tf_op jit(solution)/shard_map/ppermute | solution.py:30
  20.5 0.6 copy-done.5
  21.1 2.1 %pack_far.1 = (bf16[2,256,768]{2,1,0:T(8,128)(2,1)S(1)}, bf16[2,256,768]{2,1,0:T(8,128)(2,1)}, bf16[2,256,640]{2,1,0:T(8,128)(2,1)}, bf16[2,256,640]{2,1,0:T(8,1...) custom-call(s32[32]{0:T(128)S(1)} %copy-done.5, bf16[512,1536]{1,0:T(8,128)(2,1)S(1)} %copy-done, ...), custom_call_target="tpu_custom_call" | custom-call | tf_op jit(solution)/shard_map/pack_far/pallas_call | solution.py:240
  23.2 1.9 %collective-permute-start.5 = (bf16[2,256,768]{2,1,0:T(8,128)(2,1)S(1)}, bf16[2,256,768]{2,1,0:T(8,128)(2,1)S(1)}, u32[]{:S(2)}, u32[]{:S(2)}) collective-permute-start(bf16[2,256,768]{2,1,0:T(8,128)(2,1)S(1)} %get-tuple-element.27), channel_id=1, source_target_pairs={{0,4},{1,5},{2,6},{3,7},{4,8},{5,9},{6,10},{7,11},{8,12},{9,13},{1... | collective-permute-start | bytes 2359304 | tf_op jit(solution)/shard_map/ppermute | solution.py:30
  25.2 6.4 %collective-permute-start.6 = (bf16[2,256,768]{2,1,0:T(8,128)(2,1)}, bf16[2,256,768]{2,1,0:T(8,128)(2,1)}, u32[]{:S(2)}, u32[]{:S(2)}) collective-permute-start(bf16[2,256,768]{2,1,0:T(8,128)(2,1)} %get-tuple-element.28), channel_id=1, source_target_pairs={{4,0},{5,1},{6,2},{7,3},{8,4},{9,5},{10,6},{11,7},{12,8},{13,9},{1... | collective-permute-start | bytes 2359304 | tf_op jit(solution)/shard_map/ppermute | solution.py:30
  31.6 2.0 %collective-permute-start.7 = (bf16[2,256,640]{2,1,0:T(8,128)(2,1)}, bf16[2,256,640]{2,1,0:T(8,128)(2,1)}, u32[]{:S(2)}, u32[]{:S(2)}) collective-permute-start(bf16[2,256,640]{2,1,0:T(8,128)(2,1)} %get-tuple-element.30), channel_id=1, source_target_pairs={{0,4},{1,5},{2,6},{3,7},{4,8},{5,9},{6,10},{7,11},{8,12},{9,13},{1... | collective-permute-start | bytes 1966088 | tf_op jit(solution)/shard_map/ppermute | solution.py:30
  33.5 26.3 %collective-permute-done.5.rest_2_ = bf16[2,256,768]{2,1,0:T(8,128)(2,1)S(1)} collective-permute-done((bf16[2,256,768]{2,1,0:T(8,128)(2,1)S(1)}, bf16[2,256,768]{2,1,0:T(8,128)(2,1)S(1)}, u32[]{:S(2)}, u32[]{:S(2)}) %collective-permute-start.5) | collective-permute-done | bytes 786464 | tf_op jit(solution)/shard_map/ppermute | solution.py:30
  59.8 0.9 copy-done.3
  60.7 12.2 %collective-permute-start.8 = (bf16[2,256,640]{2,1,0:T(8,128)(2,1)}, bf16[2,256,640]{2,1,0:T(8,128)(2,1)}, u32[]{:S(2)}, u32[]{:S(2)}) collective-permute-start(bf16[2,256,640]{2,1,0:T(8,128)(2,1)} %get-tuple-element.31), channel_id=1, source_target_pairs={{4,0},{5,1},{6,2},{7,3},{8,4},{9,5},{10,6},{11,7},{12,8},{13,9},{1... | collective-permute-start | bytes 1966088 | tf_op jit(solution)/shard_map/ppermute | solution.py:30
  72.9 14.6 %collective-permute-done.6.rest_3_ = bf16[2,256,768]{2,1,0:T(8,128)(2,1)} collective-permute-done((bf16[2,256,768]{2,1,0:T(8,128)(2,1)}, bf16[2,256,768]{2,1,0:T(8,128)(2,1)}, u32[]{:S(2)}, u32[]{:S(2)}) %collective-permute-start.6) | collective-permute-done | bytes 786464 | tf_op jit(solution)/shard_map/ppermute | solution.py:30
  87.6 1.4 copy-done.2
  89.0 1.1 copy-done.4
  90.1 10.3 %shard_map.65 = (bf16[256,768]{1,0:T(8,128)(2,1)S(1)}, bf16[256,768]{1,0:T(8,128)(2,1)S(1)}) custom-call(s32[1]{0:T(128)} %bitcast.half, s32[32]{0:T(128)S(1)} %copy-done.6, bf16[512,1536]{1,0:T(8,128)(2,1)S(1)} %copy-done.2, bf16[512,1536]{1,0:T(8,128)(2,1)S(1)} %copy-done, bf16[512,1536]{1,0:T(8,128)(2,1)S(1)} %copy-done.1, ...), custom_call_target="tpu_custom_call" | custom-call | tf_op jit(solution)/shard_map/pallas_call | solution.py:259
  100.4 2.8 %collective-permute-start.9 = (bf16[256,768]{1,0:T(8,128)(2,1)S(1)}, bf16[256,768]{1,0:T(8,128)(2,1)S(1)}, u32[]{:S(2)}, u32[]{:S(2)}) collective-permute-start(bf16[256,768]{1,0:T(8,128)(2,1)S(1)} %get-tuple-element.33), channel_id=1, source_target_pairs={{0,1},{1,0},{2,3},{3,2},{4,5},{5,4},{6,7},{7,6},{8,9},{9,8},{10,11... | collective-permute-start | bytes 1179656 | tf_op jit(solution)/shard_map/ppermute | solution.py:35
  103.2 9.3 %shard_map.66 = (bf16[256,640]{1,0:T(8,128)(2,1)S(1)}, bf16[256,640]{1,0:T(8,128)(2,1)S(1)}) custom-call(s32[1]{0:T(128)} %bitcast.half, s32[32]{0:T(128)S(1)} %copy-done.6, bf16[512,1536]{1,0:T(8,128)(2,1)S(1)} %copy-done.2, bf16[512,1536]{1,0:T(8,128)(2,1)S(1)} %copy-done, bf16[512,1536]{1,0:T(8,128)(2,1)S(1)} %copy-done.1, ...), custom_call_target="tpu_custom_call" | custom-call | tf_op jit(solution)/shard_map/pallas_call | solution.py:259
  112.7 9.5 %collective-permute-start.2 = (bf16[2,256,128]{2,1,0:T(8,128)(2,1)S(1)}, bf16[2,256,128]{2,1,0:T(8,128)(2,1)S(1)}, u32[]{:S(2)}, u32[]{:S(2)}) collective-permute-start(bf16[2,256,128]{2,1,0:T(8,128)(2,1)S(1)} %get-tuple-element.23), channel_id=1, source_target_pairs={{0,4},{1,5},{2,6},{3,7},{4,8},{5,9},{6,10},{7,11},{8,12},{9,13},{1... | collective-permute-start | bytes 393224 | tf_op jit(solution)/shard_map/ppermute | solution.py:30
  122.2 20.9 %collective-permute-start.3 = (bf16[2,256,128]{2,1,0:T(8,128)(2,1)S(1)}, bf16[2,256,128]{2,1,0:T(8,128)(2,1)S(1)}, u32[]{:S(2)}, u32[]{:S(2)}) collective-permute-start(bf16[2,256,128]{2,1,0:T(8,128)(2,1)S(1)} %get-tuple-element.24), channel_id=1, source_target_pairs={{4,0},{5,1},{6,2},{7,3},{8,4},{9,5},{10,6},{11,7},{12,8},{13,9},{1... | collective-permute-start | bytes 393224 | tf_op jit(solution)/shard_map/ppermute | solution.py:30
  143.2 2.8 %collective-permute-done.2.rest_2_ = bf16[2,256,128]{2,1,0:T(8,128)(2,1)S(1)} collective-permute-done((bf16[2,256,128]{2,1,0:T(8,128)(2,1)S(1)}, bf16[2,256,128]{2,1,0:T(8,128)(2,1)S(1)}, u32[]{:S(2)}, u32[]{:S(2)}) %collective-permute-start.2) | collective-permute-done | bytes 131104 | tf_op jit(solution)/shard_map/ppermute | solution.py:30
  146.4 4.0 %shard_map.64 = (bf16[256,128]{1,0:T(8,128)(2,1)S(1)}, bf16[256,128]{1,0:T(8,128)(2,1)S(1)}) custom-call(s32[1]{0:T(128)} %bitcast.half, s32[32]{0:T(128)S(1)} %copy-done.6, bf16[512,1536]{1,0:T(8,128)(2,1)S(1)} %copy-done.2, bf16[512,1536]{1,0:T(8,128)(2,1)S(1)} %copy-done, bf16[512,1536]{1,0:T(8,128)(2,1)S(1)} %copy-done.1, ...), custom_call_target="tpu_custom_call" | custom-call | tf_op jit(solution)/shard_map/pallas_call | solution.py:259
  150.4 2.6 %collective-permute-start.4 = (bf16[256,128]{1,0:T(8,128)(2,1)S(1)}, bf16[256,128]{1,0:T(8,128)(2,1)S(1)}, u32[]{:S(2)}, u32[]{:S(2)}) collective-permute-start(bf16[256,128]{1,0:T(8,128)(2,1)S(1)} %get-tuple-element.26), channel_id=1, source_target_pairs={{0,1},{1,0},{2,3},{3,2},{4,5},{5,4},{6,7},{7,6},{8,9},{9,8},{10,11... | collective-permute-start | bytes 196616 | tf_op jit(solution)/shard_map/ppermute | solution.py:35
  153.7 1.2 shard_map.67.rest_2_
  155.0 0.7 shard_map.68
  (19 shorter events, 0.6 us)
Async XLA Ops:
  0.0 20.5 %copy-start = (bf16[512,1536]{1,0:T(8,128)(2,1)S(1)}, bf16[512,1536]{1,0:T(8,128)(2,1)}, u32[]{:S(2)}) copy-start(bf16[512,1536]{1,0:T(8,128)(2,1)} %keys.9) | copy-start | bytes 4718596
  0.0 20.5 %copy-start.1 = (bf16[512,1536]{1,0:T(8,128)(2,1)S(1)}, bf16[512,1536]{1,0:T(8,128)(2,1)}, u32[]{:S(2)}) copy-start(bf16[512,1536]{1,0:T(8,128)(2,1)} %values.9) | copy-start | bytes 4718596
  5.1 82.4 %collective-permute-start = (bf16[2,256,1536]{2,1,0:T(8,128)(2,1)}, bf16[2,256,1536]{2,1,0:T(8,128)(2,1)}, u32[]{:S(2)}, u32[]{:S(2)}) collective-permute-start(bf16[2,256,1536]{2,1,0:T(8,128)(2,1)} %get-tuple-element.21), channel_id=1, source_target_pairs={{0,2},{1,3},{2,4},{3,5},{4,6},{5,7},{6,8},{7,9},{8,10},{9,11},{10,... | collective-permute-start | bytes 4718600 | tf_op jit(solution)/shard_map/ppermute | solution.py:30
  9.6 78.0 %collective-permute-start.1 = (bf16[2,256,1536]{2,1,0:T(8,128)(2,1)}, bf16[2,256,1536]{2,1,0:T(8,128)(2,1)}, u32[]{:S(2)}, u32[]{:S(2)}) collective-permute-start(bf16[2,256,1536]{2,1,0:T(8,128)(2,1)} %get-tuple-element.22), channel_id=1, source_target_pairs={{2,0},{3,1},{4,2},{5,3},{6,4},{7,5},{8,6},{9,7},{10,8},{11,9},{12,... | collective-permute-start | bytes 4718600 | tf_op jit(solution)/shard_map/ppermute | solution.py:30
  20.5 0.7 copy-start.5
  21.1 66.4 %copy-start.6 = (s32[32]{0:T(128)S(1)}, s32[32]{0:T(128)}, u32[]{:S(2)}) copy-start(s32[32]{0:T(128)} %get-tuple-element.20.table) | copy-start | bytes 388
  23.2 36.6 %collective-permute-start.5 = (bf16[2,256,768]{2,1,0:T(8,128)(2,1)S(1)}, bf16[2,256,768]{2,1,0:T(8,128)(2,1)S(1)}, u32[]{:S(2)}, u32[]{:S(2)}) collective-permute-start(bf16[2,256,768]{2,1,0:T(8,128)(2,1)S(1)} %get-tuple-element.27), channel_id=1, source_target_pairs={{0,4},{1,5},{2,6},{3,7},{4,8},{5,9},{6,10},{7,11},{8,12},{9,13},{1... | collective-permute-start | bytes 2359304 | tf_op jit(solution)/shard_map/ppermute | solution.py:30
  25.2 62.4 %collective-permute-start.6 = (bf16[2,256,768]{2,1,0:T(8,128)(2,1)}, bf16[2,256,768]{2,1,0:T(8,128)(2,1)}, u32[]{:S(2)}, u32[]{:S(2)}) collective-permute-start(bf16[2,256,768]{2,1,0:T(8,128)(2,1)} %get-tuple-element.28), channel_id=1, source_target_pairs={{4,0},{5,1},{6,2},{7,3},{8,4},{9,5},{10,6},{11,7},{12,8},{13,9},{1... | collective-permute-start | bytes 2359304 | tf_op jit(solution)/shard_map/ppermute | solution.py:30
  31.6 71.7 %collective-permute-start.7 = (bf16[2,256,640]{2,1,0:T(8,128)(2,1)}, bf16[2,256,640]{2,1,0:T(8,128)(2,1)}, u32[]{:S(2)}, u32[]{:S(2)}) collective-permute-start(bf16[2,256,640]{2,1,0:T(8,128)(2,1)} %get-tuple-element.30), channel_id=1, source_target_pairs={{0,4},{1,5},{2,6},{3,7},{4,8},{5,9},{6,10},{7,11},{8,12},{9,13},{1... | collective-permute-start | bytes 1966088 | tf_op jit(solution)/shard_map/ppermute | solution.py:30
  59.8 0.9 copy-start.3
  60.7 42.6 %collective-permute-start.8 = (bf16[2,256,640]{2,1,0:T(8,128)(2,1)}, bf16[2,256,640]{2,1,0:T(8,128)(2,1)}, u32[]{:S(2)}, u32[]{:S(2)}) collective-permute-start(bf16[2,256,640]{2,1,0:T(8,128)(2,1)} %get-tuple-element.31), channel_id=1, source_target_pairs={{4,0},{5,1},{6,2},{7,3},{8,4},{9,5},{10,6},{11,7},{12,8},{13,9},{1... | collective-permute-start | bytes 1966088 | tf_op jit(solution)/shard_map/ppermute | solution.py:30
  87.6 1.4 copy-start.2
  89.0 1.1 copy-start.4
  100.4 53.3 %collective-permute-start.9 = (bf16[256,768]{1,0:T(8,128)(2,1)S(1)}, bf16[256,768]{1,0:T(8,128)(2,1)S(1)}, u32[]{:S(2)}, u32[]{:S(2)}) collective-permute-start(bf16[256,768]{1,0:T(8,128)(2,1)S(1)} %get-tuple-element.33), channel_id=1, source_target_pairs={{0,1},{1,0},{2,3},{3,2},{4,5},{5,4},{6,7},{7,6},{8,9},{9,8},{10,11... | collective-permute-start | bytes 1179656 | tf_op jit(solution)/shard_map/ppermute | solution.py:35
  112.5 41.2 %collective-permute-start.10 = (bf16[256,640]{1,0:T(8,128)(2,1)S(1)}, bf16[256,640]{1,0:T(8,128)(2,1)S(1)}, u32[]{:S(2)}, u32[]{:S(2)}) collective-permute-start(bf16[256,640]{1,0:T(8,128)(2,1)S(1)} %get-tuple-element.34), channel_id=1, source_target_pairs={{0,1},{1,0},{2,3},{3,2},{4,5},{5,4},{6,7},{7,6},{8,9},{9,8},{10,11... | collective-permute-start | bytes 983048 | tf_op jit(solution)/shard_map/ppermute | solution.py:35
  112.7 33.3 %collective-permute-start.2 = (bf16[2,256,128]{2,1,0:T(8,128)(2,1)S(1)}, bf16[2,256,128]{2,1,0:T(8,128)(2,1)S(1)}, u32[]{:S(2)}, u32[]{:S(2)}) collective-permute-start(bf16[2,256,128]{2,1,0:T(8,128)(2,1)S(1)} %get-tuple-element.23), channel_id=1, source_target_pairs={{0,4},{1,5},{2,6},{3,7},{4,8},{5,9},{6,10},{7,11},{8,12},{9,13},{1... | collective-permute-start | bytes 393224 | tf_op jit(solution)/shard_map/ppermute | solution.py:30
  122.2 24.2 %collective-permute-start.3 = (bf16[2,256,128]{2,1,0:T(8,128)(2,1)S(1)}, bf16[2,256,128]{2,1,0:T(8,128)(2,1)S(1)}, u32[]{:S(2)}, u32[]{:S(2)}) collective-permute-start(bf16[2,256,128]{2,1,0:T(8,128)(2,1)S(1)} %get-tuple-element.24), channel_id=1, source_target_pairs={{4,0},{5,1},{6,2},{7,3},{8,4},{9,5},{10,6},{11,7},{12,8},{13,9},{1... | collective-permute-start | bytes 393224 | tf_op jit(solution)/shard_map/ppermute | solution.py:30
  150.4 4.5 %collective-permute-start.4 = (bf16[256,128]{1,0:T(8,128)(2,1)S(1)}, bf16[256,128]{1,0:T(8,128)(2,1)S(1)}, u32[]{:S(2)}, u32[]{:S(2)}) collective-permute-start(bf16[256,128]{1,0:T(8,128)(2,1)S(1)} %get-tuple-element.26), channel_id=1, source_target_pairs={{0,1},{1,0},{2,3},{3,2},{4,5},{5,4},{6,7},{7,6},{8,9},{9,8},{10,11... | collective-permute-start | bytes 196616 | tf_op jit(solution)/shard_map/ppermute | solution.py:35

commit v2 on v1

--- a/solution.py
+++ b/solution.py
@@ -13,7 +13,8 @@
 CAP = 2
 OFFSETS = (1, -1, 2, -2)
 NEAR = 2
-CHUNKS = (6, 5, 1)
+CHUNKS = (8, 4)
+GROUP = 4
 EXP2_SCALE = HEAD_DIM ** (-0.5) * 1.4426950408889634
 VMEM_BYTES = 24 << 20
 
@@ -133,48 +134,75 @@
                     ]
 
 
-def attend_tile(queries, pool, result, slots, rows, begin, heads):
-    for head in heads:
-        cols = slice(head * HEAD_DIM, (head + 1) * HEAD_DIM)
-        query = queries[rows, begin + head * HEAD_DIM : begin + (head + 1) * HEAD_DIM]
-        keys = jnp.concatenate([pool[0, slot, cols] for slot in slots], axis=0)
-        values = jnp.concatenate([pool[1, slot, cols] for slot in slots], axis=0)
-        scores = lax.dot_general(
-            query, keys, (((1,), (1,)), ((), ())), preferred_element_type=jnp.float32
+def attend_tile(query_ref, pool, result, slots, rows, heads):
+    cols = [slice(head * HEAD_DIM, (head + 1) * HEAD_DIM) for head in heads]
+    scores, weights, totals, mixed = [], [], [], []
+    for col in cols:
+        keys = jnp.concatenate([pool[0, slot, col] for slot in slots], axis=0)
+        scores.append(
+            lax.dot_general(
+                query_ref[rows, col],
+                keys,
+                (((1,), (1,)), ((), ())),
+                preferred_element_type=jnp.float32,
+            )
         )
-        top = jnp.max(scores, axis=1, keepdims=True)
-        weights = jnp.exp2((scores - top) * EXP2_SCALE)
-        total = jnp.sum(weights, axis=1, keepdims=True)
-        mixed = jnp.dot(weights.astype(jnp.bfloat16), values, preferred_element_type=jnp.float32)
-        result[rows, cols] = (mixed / total).astype(jnp.bfloat16)
+    tops = [jnp.max(score, axis=1, keepdims=True) for score in scores]
+    for score, top in zip(scores, tops):
+        weight = jnp.exp2((score - top) * EXP2_SCALE)
+        totals.append(jnp.sum(weight, axis=1, keepdims=True))
+        weights.append(weight.astype(jnp.bfloat16))
+    for weight, col in zip(weights, cols):
+        values = jnp.concatenate([pool[1, slot, col] for slot in slots], axis=0)
+        mixed.append(jnp.dot(weight, values, preferred_element_type=jnp.float32))
+    for mix, total, col in zip(mixed, totals, cols):
+        result[rows, col] = (mix / total).astype(jnp.bfloat16)
+
+
+def warm_kernel(table, queries, out):
+    del queries
+    for index in range(table.shape[0]):
+        out[index] = table[index]
 
 
 def attend_kernel(begin, heads, picks, half, table, queries, keys, values, *rest):
-    lands, (sent, kept, pool, result) = rest[:4], rest[4:]
+    lands, (sent, kept, query_ref, pool, result, sems) = rest[:4], rest[4:]
     tokens = queries.shape[0]
     tiles_dev = tokens // TILE
     span = CAP * TILE
     width = heads * HEAD_DIM
-    pool[0, :tokens, :] = keys[:, begin : begin + width]
-    pool[1, :tokens, :] = values[:, begin : begin + width]
+    cols = pl.ds(begin, width)
+    copies = [
+        pltpu.make_async_copy(queries.at[:, cols], query_ref, sems.at[0]),
+        pltpu.make_async_copy(keys.at[:, cols], pool.at[0, pl.ds(0, tokens), :], sems.at[1]),
+        pltpu.make_async_copy(values.at[:, cols], pool.at[1, pl.ds(0, tokens), :], sems.at[2]),
+    ]
     for index, land in enumerate(lands):
-        at = begin if index < NEAR else 0
-        pool[:, tokens + index * span : tokens + (index + 1) * span, :] = land[
-            :, :, at : at + width
-        ]
+        part = cols if index < NEAR else pl.ds(0, width)
+        copies.append(
+            pltpu.make_async_copy(
+                land.at[:, :, part],
+                pool.at[:, pl.ds(tokens + index * span, span), :],
+                sems.at[3 + index],
+            )
+        )
+    for copy in copies:
+        copy.start()
+    for copy in copies:
+        copy.wait()
 
     def one_tile(tile, carry):
-        rows = pl.ds(pl.multiple_of(tile * TILE, TILE), TILE)
-        slots = [
-            pl.ds(pl.multiple_of(table[tile * picks + pick] * TILE, TILE), TILE)
-            for pick in range(picks)
-        ]
+        rows = tile_rows(tile)
+        slots = [tile_rows(table[tile * picks + pick]) for pick in range(picks)]
         live = table[tiles_dev * picks + tile]
         for count in range(2, picks + 1):
 
             @pl.when(live == count)
             def _(count=count):
-                attend_tile(queries, pool, result, slots[:count], rows, begin, range(heads))
+                for group in range(0, heads, GROUP):
+                    attend_tile(
+                        query_ref, pool, result, slots[:count], rows, range(group, group + GROUP)
+                    )
 
         return carry
 
@@ -254,16 +282,27 @@
             + [shifted(piece, "seq", 2 * off) for piece, off in zip(pieces, OFFSETS[NEAR:])]
         )
 
+    table = pl.pallas_call(
+        warm_kernel,
+        out_shape=jax.ShapeDtypeStruct(table.shape, table.dtype),
+        in_specs=[SMEM, VMEM],
+        out_specs=SMEM,
+        compiler_params=PARAMS,
+        name="warm_queries",
+    )(table, query_rows)
+
     kept_all, their_all = [], []
     for index, (begin, width, heads) in enumerate(zip(begins, widths, CHUNKS)):
         sent, kept = pl.pallas_call(
             functools.partial(attend_kernel, begin, heads, picks),
             out_shape=[jax.ShapeDtypeStruct((half_rows, width), dtype)] * 2,
-            in_specs=[SMEM, SMEM] + [VMEM] * 7,
+            in_specs=[SMEM, SMEM] + [HBM] * 7,
             out_specs=[VMEM, VMEM],
             scratch_shapes=[
+                pltpu.VMEM((tokens, width), dtype),
                 pltpu.VMEM((2, tokens + len(OFFSETS) * span, width), dtype),
                 pltpu.VMEM((tokens, width), dtype),
+                pltpu.SemaphoreType.DMA((3 + len(OFFSETS),)),
             ],
             compiler_params=PARAMS,
         )(my_half, table, query_rows, key_rows, value_rows, *landed[index])

time: 156 us -> 140 us (0.90)
  the two profiles are of different devices: /device:TPU:647 before, /device:TPU:539 now
where the time goes in v2:
time: 140 us; the launch traced here: 139 us
  waiting for transfers between devices  78.5 us (56%)
  starting transfers between devices  32.8 us (23%)
  Pallas kernels  21.5 us (15%)
  local copies, waits for them, and re-layouts  5.78 us (4%)
    ppermute x6, waiting for transfers between devices, shifted(): return lax.ppermute(block, axis, route)  78.5 us
    ppermute x6, starting transfers between devices, shifted(): return lax.ppermute(block, axis, route)  29.6 us
    pallas_call x2, Pallas kernels, body(): pl.pallas_call(functools.partial(attend_kernel, begin, heads, picks), out...  11.3 us
    unnamed x16, local copies, waits for them, and re-layouts  5.78 us
    pallas_call x1, Pallas kernels, body(): pl.pallas_call(functools.partial(pack_near_kernel, (tiles_dev, picks, sha...  5.13 us
    ppermute x2, starting transfers between devices, partner(): return lax.ppermute(block, axis, route)  3.16 us
  transfers between devices with their start and end apart: 8, of which 1 were waited for; matrix products, arithmetic and copies ran while one was open for 0% of the time, Pallas kernels for 11%

profile of v2, /device:TPU:539, one launch (start us, length us, event | category | flops | bytes accessed | tf_op | source)
XLA Modules:
  0.0 139.4 jit_solution(13408658556713954450)
XLA Ops:
  0.0 5.1 %pack_near.1 = (s32[32]{0:T(128)}, bf16[2,256,1536]{2,1,0:T(8,128)(2,1)}, bf16[2,256,1536]{2,1,0:T(8,128)(2,1)}) custom-call(s32[1]{0:T(128)} %bitcast.1.me, s32[6,256]{1,0:T(8,128)} %bitcast.3, s32[256]{0:T(256)} %counts.1, bf16[512,1536]{1,0:T(8,128)(2,1)} %keys.7, bf16[512,1536]{1,0:T(8,128)(2,1)} %values.7), custom_call_target="tpu_custom_call" | custom-call | tf_op jit(solution)/shard_map/pack_near/pallas_call | solution.py:255
  5.1 4.4 %collective-permute-start = (bf16[2,256,1536]{2,1,0:T(8,128)(2,1)}, bf16[2,256,1536]{2,1,0:T(8,128)(2,1)}, u32[]{:S(2)}, u32[]{:S(2)}) collective-permute-start(bf16[2,256,1536]{2,1,0:T(8,128)(2,1)} %get-tuple-element.17), channel_id=1, source_target_pairs={{0,2},{1,3},{2,4},{3,5},{4,6},{5,7},{6,8},{7,9},{8,10},{9,11},{10,... | collective-permute-start | bytes 4718600 | tf_op jit(solution)/shard_map/ppermute | solution.py:31
  9.6 2.0 %collective-permute-start.1 = (bf16[2,256,1536]{2,1,0:T(8,128)(2,1)}, bf16[2,256,1536]{2,1,0:T(8,128)(2,1)}, u32[]{:S(2)}, u32[]{:S(2)}) collective-permute-start(bf16[2,256,1536]{2,1,0:T(8,128)(2,1)} %get-tuple-element.18), channel_id=1, source_target_pairs={{2,0},{3,1},{4,2},{5,3},{6,4},{7,5},{8,6},{9,7},{10,8},{11,9},{12,... | collective-permute-start | bytes 4718600 | tf_op jit(solution)/shard_map/ppermute | solution.py:31
  11.6 0.7 copy-done.6
  12.3 2.0 %pack_far.1 = (bf16[2,256,1024]{2,1,0:T(8,128)(2,1)S(1)}, bf16[2,256,1024]{2,1,0:T(8,128)(2,1)}, bf16[2,256,512]{2,1,0:T(8,128)(2,1)}, bf16[2,256,512]{2,1,0:T(8,128)(2,1)}) custom-call(s32[32]{0:T(128)S(1)} %copy-done.6, bf16[512,1536]{1,0:T(8,128)(2,1)S(1)} %copy-done, bf16[512,1536]{1,0:T(8,128)(2,1)S(1)} %copy-done.1), custom_call_target="tpu_custom_call" | custom-call | tf_op jit(solution)/shard_map/pack_far/pallas_call | solution.py:268
  14.3 7.8 %collective-permute-start.5 = (bf16[2,256,1024]{2,1,0:T(8,128)(2,1)S(1)}, bf16[2,256,1024]{2,1,0:T(8,128)(2,1)S(1)}, u32[]{:S(2)}, u32[]{:S(2)}) collective-permute-start(bf16[2,256,1024]{2,1,0:T(8,128)(2,1)S(1)} %get-tuple-element.23), channel_id=1, source_target_pairs={{0,4},{1,5},{2,6},{3,7},{4,8},{5,9},{6,10},{7,11},{8,12},{9,13},{1... | collective-permute-start | bytes 3145736 | tf_op jit(solution)/shard_map/ppermute | solution.py:31
  22.1 6.0 %collective-permute-start.6 = (bf16[2,256,1024]{2,1,0:T(8,128)(2,1)}, bf16[2,256,1024]{2,1,0:T(8,128)(2,1)}, u32[]{:S(2)}, u32[]{:S(2)}) collective-permute-start(bf16[2,256,1024]{2,1,0:T(8,128)(2,1)} %get-tuple-element.24), channel_id=1, source_target_pairs={{4,0},{5,1},{6,2},{7,3},{8,4},{9,5},{10,6},{11,7},{12,8},{13,9},{1... | collective-permute-start | bytes 3145736 | tf_op jit(solution)/shard_map/ppermute | solution.py:31
  28.1 2.0 %collective-permute-start.2 = (bf16[2,256,512]{2,1,0:T(8,128)(2,1)}, bf16[2,256,512]{2,1,0:T(8,128)(2,1)}, u32[]{:S(2)}, u32[]{:S(2)}) collective-permute-start(bf16[2,256,512]{2,1,0:T(8,128)(2,1)} %get-tuple-element.19), channel_id=1, source_target_pairs={{0,4},{1,5},{2,6},{3,7},{4,8},{5,9},{6,10},{7,11},{8,12},{9,13},{1... | collective-permute-start | bytes 1572872 | tf_op jit(solution)/shard_map/ppermute | solution.py:31
  30.1 78.5 %collective-permute-done.5.rest_2_ = bf16[2,256,1024]{2,1,0:T(8,128)(2,1)S(1)} collective-permute-done((bf16[2,256,1024]{2,1,0:T(8,128)(2,1)S(1)}, bf16[2,256,1024]{2,1,0:T(8,128)(2,1)S(1)}, u32[]{:S(2)}, u32[]{:S(2)}) %collective-permute-start.5) | collective-permute-done | bytes 1048608 | tf_op jit(solution)/shard_map/ppermute | solution.py:31
  108.6 1.1 copy-done.4
  109.6 7.4 %collective-permute-start.3 = (bf16[2,256,512]{2,1,0:T(8,128)(2,1)}, bf16[2,256,512]{2,1,0:T(8,128)(2,1)}, u32[]{:S(2)}, u32[]{:S(2)}) collective-permute-start(bf16[2,256,512]{2,1,0:T(8,128)(2,1)} %get-tuple-element.20), channel_id=1, source_target_pairs={{4,0},{5,1},{6,2},{7,3},{8,4},{9,5},{10,6},{11,7},{12,8},{13,9},{1... | collective-permute-start | bytes 1572872 | tf_op jit(solution)/shard_map/ppermute | solution.py:31
  117.1 0.0 copy-start.2
  117.1 1.4 %copy-done.2 = bf16[512,1536]{1,0:T(8,128)(2,1)S(1)} copy-done((bf16[512,1536]{1,0:T(8,128)(2,1)S(1)}, bf16[512,1536]{1,0:T(8,128)(2,1)}, u32[]{:S(2)}) %copy-start.2) | copy-done | bytes 1572888
  118.5 1.2 warm_queries.1.table
  119.7 0.0 collective-permute-done.6.rest_3_
  119.7 0.0 copy-start.3
  119.7 1.4 %copy-done.3 = bf16[512,1536]{1,0:T(8,128)(2,1)S(1)} copy-done((bf16[512,1536]{1,0:T(8,128)(2,1)S(1)}, bf16[512,1536]{1,0:T(8,128)(2,1)}, u32[]{:S(2)}) %copy-start.3) | copy-done | bytes 1572888
  121.1 1.2 copy-done.5
  122.3 6.8 %shard_map.65 = (bf16[256,1024]{1,0:T(8,128)(2,1)S(1)}, bf16[256,1024]{1,0:T(8,128)(2,1)S(1)}) custom-call(s32[1]{0:T(128)} %bitcast.half, s32[32]{0:T(128)S(1)} %warm_queries.1.table, bf16[512,1536]{1,0:T(8,128)(2,1)S(1)} %copy-done.3, bf16[512,1536]{1,0:T(8,128)(2,1)S(1)} %copy-done, bf16[512,1536]{1,0:T(8,128)(2,1)S(1)} %copy-done.1, ...), custom_call_target="tpu_custom_call" | custom-call | tf_op jit(solution)/shard_map/pallas_call | solution.py:296
  129.2 3.0 %collective-permute-start.7 = (bf16[256,1024]{1,0:T(8,128)(2,1)S(1)}, bf16[256,1024]{1,0:T(8,128)(2,1)S(1)}, u32[]{:S(2)}, u32[]{:S(2)}) collective-permute-start(bf16[256,1024]{1,0:T(8,128)(2,1)S(1)} %get-tuple-element.26), channel_id=1, source_target_pairs={{0,1},{1,0},{2,3},{3,2},{4,5},{5,4},{6,7},{7,6},{8,9},{9,8},{10,11... | collective-permute-start | bytes 1572872 | tf_op jit(solution)/shard_map/ppermute | solution.py:36
  132.2 4.5 %shard_map.64 = (bf16[256,512]{1,0:T(8,128)(2,1)S(1)}, bf16[256,512]{1,0:T(8,128)(2,1)S(1)}) custom-call(s32[1]{0:T(128)} %bitcast.half, s32[32]{0:T(128)S(1)} %warm_queries.1.table, bf16[512,1536]{1,0:T(8,128)(2,1)S(1)} %copy-done.3, bf16[512,1536]{1,0:T(8,128)(2,1)S(1)} %copy-done, bf16[512,1536]{1,0:T(8,128)(2,1)S(1)} %copy-done.1, ...), custom_call_target="tpu_custom_call" | custom-call | tf_op jit(solution)/shard_map/pallas_call | solution.py:296
  136.7 0.2 collective-permute-start.4
  137.5 1.1 shard_map.66.rest_2_
  138.6 0.8 shard_map.67
  (15 shorter events, 0.0 us)
Async XLA Ops:
  0.0 11.5 %copy-start = (bf16[512,1536]{1,0:T(8,128)(2,1)S(1)}, bf16[512,1536]{1,0:T(8,128)(2,1)}, u32[]{:S(2)}) copy-start(bf16[512,1536]{1,0:T(8,128)(2,1)} %keys.7) | copy-start | bytes 4718596
  0.0 11.6 %copy-start.1 = (bf16[512,1536]{1,0:T(8,128)(2,1)S(1)}, bf16[512,1536]{1,0:T(8,128)(2,1)}, u32[]{:S(2)}) copy-start(bf16[512,1536]{1,0:T(8,128)(2,1)} %values.7) | copy-start | bytes 4718596
  5.1 114.5 %collective-permute-start = (bf16[2,256,1536]{2,1,0:T(8,128)(2,1)}, bf16[2,256,1536]{2,1,0:T(8,128)(2,1)}, u32[]{:S(2)}, u32[]{:S(2)}) collective-permute-start(bf16[2,256,1536]{2,1,0:T(8,128)(2,1)} %get-tuple-element.17), channel_id=1, source_target_pairs={{0,2},{1,3},{2,4},{3,5},{4,6},{5,7},{6,8},{7,9},{8,10},{9,11},{10,... | collective-permute-start | bytes 4718600 | tf_op jit(solution)/shard_map/ppermute | solution.py:31
  9.6 110.1 %collective-permute-start.1 = (bf16[2,256,1536]{2,1,0:T(8,128)(2,1)}, bf16[2,256,1536]{2,1,0:T(8,128)(2,1)}, u32[]{:S(2)}, u32[]{:S(2)}) collective-permute-start(bf16[2,256,1536]{2,1,0:T(8,128)(2,1)} %get-tuple-element.18), channel_id=1, source_target_pairs={{2,0},{3,1},{4,2},{5,3},{6,4},{7,5},{8,6},{9,7},{10,8},{11,9},{12,... | collective-permute-start | bytes 4718600 | tf_op jit(solution)/shard_map/ppermute | solution.py:31
  11.6 0.7 copy-start.6
  12.3 104.8 %copy-start.7 = (s32[32]{0:T(128)S(1)}, s32[32]{0:T(128)}, u32[]{:S(2)}) copy-start(s32[32]{0:T(128)} %get-tuple-element.16.table) | copy-start | bytes 388
  14.3 94.3 %collective-permute-start.5 = (bf16[2,256,1024]{2,1,0:T(8,128)(2,1)S(1)}, bf16[2,256,1024]{2,1,0:T(8,128)(2,1)S(1)}, u32[]{:S(2)}, u32[]{:S(2)}) collective-permute-start(bf16[2,256,1024]{2,1,0:T(8,128)(2,1)S(1)} %get-tuple-element.23), channel_id=1, source_target_pairs={{0,4},{1,5},{2,6},{3,7},{4,8},{5,9},{6,10},{7,11},{8,12},{9,13},{1... | collective-permute-start | bytes 3145736 | tf_op jit(solution)/shard_map/ppermute | solution.py:31
  22.1 97.6 %collective-permute-start.6 = (bf16[2,256,1024]{2,1,0:T(8,128)(2,1)}, bf16[2,256,1024]{2,1,0:T(8,128)(2,1)}, u32[]{:S(2)}, u32[]{:S(2)}) collective-permute-start(bf16[2,256,1024]{2,1,0:T(8,128)(2,1)} %get-tuple-element.24), channel_id=1, source_target_pairs={{4,0},{5,1},{6,2},{7,3},{8,4},{9,5},{10,6},{11,7},{12,8},{13,9},{1... | collective-permute-start | bytes 3145736 | tf_op jit(solution)/shard_map/ppermute | solution.py:31
  28.1 104.0 %collective-permute-start.2 = (bf16[2,256,512]{2,1,0:T(8,128)(2,1)}, bf16[2,256,512]{2,1,0:T(8,128)(2,1)}, u32[]{:S(2)}, u32[]{:S(2)}) collective-permute-start(bf16[2,256,512]{2,1,0:T(8,128)(2,1)} %get-tuple-element.19), channel_id=1, source_target_pairs={{0,4},{1,5},{2,6},{3,7},{4,8},{5,9},{6,10},{7,11},{8,12},{9,13},{1... | collective-permute-start | bytes 1572872 | tf_op jit(solution)/shard_map/ppermute | solution.py:31
  108.6 1.1 copy-start.4
  109.6 22.5 %collective-permute-start.3 = (bf16[2,256,512]{2,1,0:T(8,128)(2,1)}, bf16[2,256,512]{2,1,0:T(8,128)(2,1)}, u32[]{:S(2)}, u32[]{:S(2)}) collective-permute-start(bf16[2,256,512]{2,1,0:T(8,128)(2,1)} %get-tuple-element.20), channel_id=1, source_target_pairs={{4,0},{5,1},{6,2},{7,3},{8,4},{9,5},{10,6},{11,7},{12,8},{13,9},{1... | collective-permute-start | bytes 1572872 | tf_op jit(solution)/shard_map/ppermute | solution.py:31
  117.1 1.4 %copy-start.2 = (bf16[512,1536]{1,0:T(8,128)(2,1)S(1)}, bf16[512,1536]{1,0:T(8,128)(2,1)}, u32[]{:S(2)}) copy-start(bf16[512,1536]{1,0:T(8,128)(2,1)} %queries.5) | copy-start | bytes 4718596
  119.7 1.4 %copy-start.3 = (bf16[512,1536]{1,0:T(8,128)(2,1)S(1)}, bf16[512,1536]{1,0:T(8,128)(2,1)}, u32[]{:S(2)}) copy-start(bf16[512,1536]{1,0:T(8,128)(2,1)} %queries.5) | copy-start | bytes 4718596
  121.1 1.2 copy-start.5
  129.2 8.3 %collective-permute-start.7 = (bf16[256,1024]{1,0:T(8,128)(2,1)S(1)}, bf16[256,1024]{1,0:T(8,128)(2,1)S(1)}, u32[]{:S(2)}, u32[]{:S(2)}) collective-permute-start(bf16[256,1024]{1,0:T(8,128)(2,1)S(1)} %get-tuple-element.26), channel_id=1, source_target_pairs={{0,1},{1,0},{2,3},{3,2},{4,5},{5,4},{6,7},{7,6},{8,9},{9,8},{10,11... | collective-permute-start | bytes 1572872 | tf_op jit(solution)/shard_map/ppermute | solution.py:36
  136.7 1.9 %collective-permute-start.4 = (bf16[256,512]{1,0:T(8,128)(2,1)S(1)}, bf16[256,512]{1,0:T(8,128)(2,1)S(1)}, u32[]{:S(2)}, u32[]{:S(2)}) collective-permute-start(bf16[256,512]{1,0:T(8,128)(2,1)S(1)} %get-tuple-element.22), channel_id=1, source_target_pairs={{0,1},{1,0},{2,3},{3,2},{4,5},{5,4},{6,7},{7,6},{8,9},{9,8},{10,11... | collective-permute-start | bytes 786440 | tf_op jit(solution)/shard_map/ppermute | solution.py:36

commit v3 on v2

--- a/solution.py
+++ b/solution.py
@@ -54,7 +54,7 @@
     return bits
 
 
-def fill_table(my_shard, tiles, select, counts, table, tiles_dev, picks):
+def fill_table(my_shard, select, counts, table, tiles_dev, picks):
     bits = wanted_bits(select, counts, my_shard, tiles_dev, picks)
     for row in range(tiles_dev):
         line = my_shard * tiles_dev + row
@@ -70,8 +70,6 @@
             block = 2 * (jnp.abs(away) - 1) + jnp.where(away < 0, 0, 1)
             slot = jnp.where(away == 0, within, tiles_dev + block * CAP + rank)
             table[row * picks + pick] = slot
-    for index, tile in enumerate(tiles):
-        table[tiles_dev * (picks + 1) + index] = tile
 
 
 def sent_tiles(my_shard, offset, select, counts, tiles_dev, picks, shards):
@@ -85,9 +83,9 @@
     return pl.ds(pl.multiple_of(tile * TILE, TILE), TILE)
 
 
-def pack_near_kernel(sizes, me, select, counts, keys, values, table, *rest):
+def pack_near_kernel(sizes, select, counts, keys, values, *rest):
     outs, (stage, load_sems, sems) = rest[:NEAR], rest[NEAR:]
-    my_shard = me[0] // 2
+    my_shard = lax.axis_index("seq") // 2
     loads = []
     for which, rows in enumerate((keys, values)):
         for tile in range(sizes[0]):
@@ -113,25 +111,25 @@
                 )
                 copy.start()
                 copies.append(copy)
-    tiles = []
-    for offset in OFFSETS[NEAR:]:
-        tiles += sent_tiles(my_shard, offset, select, counts, *sizes)
-    fill_table(my_shard, tiles, select, counts, table, *sizes[:2])
     for copy in copies:
         copy.wait()
 
 
-def pack_far_kernel(first, begins, widths, table, keys, values, *outs):
-    far = len(OFFSETS) - NEAR
+def pack_far_kernel(sizes, begins, widths, select, counts, keys, values, near, table, *outs):
+    del near
+    my_shard = lax.axis_index("seq") // 2
+    chosen = []
+    for offset in OFFSETS[NEAR:]:
+        chosen.append(sent_tiles(my_shard, offset, select, counts, *sizes))
     for index, (begin, width) in enumerate(zip(begins, widths)):
-        for place in range(far):
-            out = outs[index * far + place]
-            for slot in range(CAP):
-                rows = tile_rows(table[first + place * CAP + slot])
+        for place, tiles in enumerate(chosen):
+            out = outs[index * len(chosen) + place]
+            for slot, tile in enumerate(tiles):
                 for which, source in enumerate((keys, values)):
                     out[which, slot * TILE : (slot + 1) * TILE, :] = source[
-                        rows, begin : begin + width
+                        tile_rows(tile), begin : begin + width
                     ]
+    fill_table(my_shard, select, counts, table, *sizes[:2])
 
 
 def attend_tile(query_ref, pool, result, slots, rows, heads):
@@ -165,7 +163,7 @@
         out[index] = table[index]
 
 
-def attend_kernel(begin, heads, picks, half, table, queries, keys, values, *rest):
+def attend_kernel(begin, heads, picks, table, queries, keys, values, *rest):
     lands, (sent, kept, query_ref, pool, result, sems) = rest[:4], rest[4:]
     tokens = queries.shape[0]
     tiles_dev = tokens // TILE
@@ -208,15 +206,15 @@
 
     lax.fori_loop(0, tiles_dev, one_tile, 0)
     half_rows = tokens // 2
-    my_half = half[0]
+    my_half = lax.axis_index("seq") % 2
     sent[...] = result[pl.ds(pl.multiple_of((1 - my_half) * half_rows, half_rows), half_rows), :]
     kept[...] = result[pl.ds(pl.multiple_of(my_half * half_rows, half_rows), half_rows), :]
 
 
-def combine_kernel(begin, count, aliased, half, guide, *rest):
+def combine_kernel(begin, count, aliased, guide, *rest):
     pieces, rest = rest[: 2 * count], rest[2 * count + aliased :]
     out, mixed, sem = rest
-    conditional = half[0] == 0
+    conditional = lax.axis_index("seq") % 2 == 0
     guidance = guide[0]
     at = 0
     for index in range(count):
@@ -234,8 +232,6 @@
 
 def body(query_rows, key_rows, value_rows, select, counts, guide_scale):
     shards = lax.axis_size("seq") // 2
-    me = lax.axis_index("seq").astype(jnp.int32)
-    my_half = (me % 2).reshape(1)
     tokens, row_width = query_rows.shape
     tiles_dev = tokens // TILE
     picks = select.shape[1]
@@ -251,28 +247,31 @@
     def box(width):
         return jax.ShapeDtypeStruct((2, span, width), dtype)
 
-    table_size = tiles_dev * (picks + 1) + far * CAP
-    table, *packed = pl.pallas_call(
-        functools.partial(pack_near_kernel, (tiles_dev, picks, shards)),
-        out_shape=[jax.ShapeDtypeStruct((table_size,), jnp.int32)] + [box(row_width)] * NEAR,
-        in_specs=[SMEM, SMEM, SMEM, HBM, HBM],
-        out_specs=[SMEM] + [HBM] * NEAR,
+    sizes = (tiles_dev, picks, shards)
+    packed = pl.pallas_call(
+        functools.partial(pack_near_kernel, sizes),
+        out_shape=[box(row_width)] * NEAR,
+        in_specs=[SMEM, SMEM, HBM, HBM],
+        out_specs=[HBM] * NEAR,
         scratch_shapes=[
             pltpu.VMEM((2, tokens, row_width), dtype),
             pltpu.SemaphoreType.DMA((2 * tiles_dev,)),
             pltpu.SemaphoreType.DMA((NEAR * CAP * 2,)),
         ],
         name="pack_near",
-    )(me.reshape(1), select.T, counts, key_rows, value_rows)
-    near = [shifted(piece, "seq", 2 * off) for piece, off in zip(packed, OFFSETS)]
-    packed = pl.pallas_call(
-        functools.partial(pack_far_kernel, tiles_dev * (picks + 1), begins, widths),
-        out_shape=[box(width) for width in widths for _ in range(far)],
-        in_specs=[SMEM, VMEM, VMEM],
-        out_specs=[VMEM] * (chunks * far),
+    )(select.T, counts, key_rows, value_rows)
+    near = []
+    for piece, offset in zip(packed, OFFSETS):
+        near.append(shifted(piece, "seq", 2 * offset))
+    table, *packed = pl.pallas_call(
+        functools.partial(pack_far_kernel, sizes, begins, widths),
+        out_shape=[jax.ShapeDtypeStruct((tiles_dev * (picks + 1),), jnp.int32)]
+        + [box(width) for width in widths for _ in range(far)],
+        in_specs=[SMEM, SMEM, VMEM, VMEM, HBM],
+        out_specs=[SMEM] + [VMEM] * (chunks * far),
         compiler_params=PARAMS,
         name="pack_far",
-    )(table, key_rows, value_rows)
+    )(select.T, counts, key_rows, value_rows, packed[0])
 
     landed = []
     for index in range(chunks):
@@ -296,7 +295,7 @@
         sent, kept = pl.pallas_call(
             functools.partial(attend_kernel, begin, heads, picks),
             out_shape=[jax.ShapeDtypeStruct((half_rows, width), dtype)] * 2,
-            in_specs=[SMEM, SMEM] + [HBM] * 7,
+            in_specs=[SMEM] + [HBM] * 7,
             out_specs=[VMEM, VMEM],
             scratch_shapes=[
                 pltpu.VMEM((tokens, width), dtype),
@@ -305,7 +304,7 @@
                 pltpu.SemaphoreType.DMA((3 + len(OFFSETS),)),
             ],
             compiler_params=PARAMS,
-        )(my_half, table, query_rows, key_rows, value_rows, *landed[index])
+        )(table, query_rows, key_rows, value_rows, *landed[index])
         kept_all.append(kept)
         their_all.append(partner(sent, "seq"))
 
@@ -317,15 +316,15 @@
         guided = pl.pallas_call(
             functools.partial(combine_kernel, begins[first], last - first, len(aliased)),
             out_shape=jax.ShapeDtypeStruct((half_rows, row_width), dtype),
-            in_specs=[SMEM, SMEM] + [VMEM] * len(pieces) + [HBM] * len(aliased),
+            in_specs=[SMEM] + [VMEM] * len(pieces) + [HBM] * len(aliased),
             out_specs=HBM,
             scratch_shapes=[
                 pltpu.VMEM((half_rows, sum(widths[first:last])), dtype),
                 pltpu.SemaphoreType.DMA,
             ],
-            input_output_aliases={2 + len(pieces): 0} if aliased else {},
+            input_output_aliases={1 + len(pieces): 0} if aliased else {},
             compiler_params=PARAMS,
-        )(my_half, guide_scale, *pieces, *aliased)
+        )(guide_scale, *pieces, *aliased)
     return guided
 
 

time: 140 us -> 137 us (0.979)
  the two profiles are of different devices: /device:TPU:539 before, /device:TPU:671 now
where the time goes in v3:
time: 137 us
  waiting for transfers between devices  80.6 us (59%)
  starting transfers between devices  33.7 us (25%)
  Pallas kernels  20.1 us (15%)
  local copies, waits for them, and re-layouts  1.43 us (1%)
    ppermute x6, waiting for transfers between devices, shifted(): return lax.ppermute(block, axis, route)  80.6 us
    ppermute x6, starting transfers between devices, shifted(): return lax.ppermute(block, axis, route)  26.4 us
    pallas_call x2, Pallas kernels, body(): pl.pallas_call(functools.partial(attend_kernel, begin, heads, picks), out...  10.5 us
    ppermute x2, starting transfers between devices, partner(): return lax.ppermute(block, axis, route)  7.37 us
    pallas_call x1, Pallas kernels, body(): pl.pallas_call(functools.partial(pack_near_kernel, sizes), out_shape=[box...  4.56 us
  transfers between devices with their start and end apart: 8, of which 1 were waited for; matrix products, arithmetic and copies ran while one was open for 0% of the time, Pallas kernels for 11%

profile of v3, /device:TPU:671, one launch (start us, length us, event | category | flops | bytes accessed | tf_op | source)
XLA Modules:
  0.0 136.8 jit_solution(6765765130285035044)
XLA Ops:
  0.0 4.6 %pack_near.1 = (bf16[2,256,1536]{2,1,0:T(8,128)(2,1)}, bf16[2,256,1536]{2,1,0:T(8,128)(2,1)}) custom-call(s32[6,256]{1,0:T(8,128)} %bitcast.1, s32[256]{0:T(256)} %counts.3, bf16[512,1536]{1,0:T(8,128)(2,1)} %keys.7, bf16[512,1536]{1,0:T(8,128)(2,1)} %values.7), custom_call_target="tpu_custom_call" | custom-call | tf_op jit(solution)/shard_map/pack_near/pallas_call | solution.py:251
  4.6 2.0 %collective-permute-start.1 = (bf16[2,256,1536]{2,1,0:T(8,128)(2,1)}, bf16[2,256,1536]{2,1,0:T(8,128)(2,1)S(1)}, u32[]{:S(2)}, u32[]{:S(2)}) collective-permute-start(bf16[2,256,1536]{2,1,0:T(8,128)(2,1)} %get-tuple-element.18), channel_id=1, source_target_pairs={{2,0},{3,1},{4,2},{5,3},{6,4},{7,5},{8,6},{9,7},{10,8},{11,9},{12,... | collective-permute-start | bytes 4718600 | tf_op jit(solution)/shard_map/ppermute | solution.py:31
  6.5 0.0 copy-start.2
  6.6 4.6 %collective-permute-start = (bf16[2,256,1536]{2,1,0:T(8,128)(2,1)}, bf16[2,256,1536]{2,1,0:T(8,128)(2,1)S(1)}, u32[]{:S(2)}, u32[]{:S(2)}) collective-permute-start(bf16[2,256,1536]{2,1,0:T(8,128)(2,1)} %get-tuple-element.16.near), channel_id=1, source_target_pairs={{0,2},{1,3},{2,4},{3,5},{4,6},{5,7},{6,8},{7,9},{8,10},{9,11},{10,... | collective-permute-start | bytes 4718600 | tf_op jit(solution)/shard_map/ppermute | solution.py:31
  11.2 1.4 %copy-done.3 = bf16[2,256,1536]{2,1,0:T(8,128)(2,1)S(1)} copy-done((bf16[2,256,1536]{2,1,0:T(8,128)(2,1)S(1)}, bf16[2,256,1536]{2,1,0:T(8,128)(2,1)}, u32[]{:S(2)}) %copy-start.3) | copy-done | bytes 1572888
  12.6 2.0 %pack_far.1 = (s32[28]{0:T(128)S(1)}, bf16[2,256,1024]{2,1,0:T(8,128)(2,1)S(1)}, bf16[2,256,1024]{2,1,0:T(8,128)(2,1)S(1)}, bf16[2,256,512]{2,1,0:T(8,128)(2,1)S(1)}, bf16[2,256,512]{2,1,0:T(8,128)(2,1)S(1)}) custom-call(s32[6,256]{1,0:T(8,128)S(1)} %bitcast.2, s32[256]{0:T(256)S(1)} %copy-done.5, bf16[512,1536]{1,0:T(8,128)(2,1)S(1)} %copy-done, ...), custom_call_target="tpu_custom_call" | custom-call | tf_op jit(solution)/shard_map/pack_far/pallas_call | solution.py:266
  14.6 7.9 %collective-permute-start.5 = (bf16[2,256,1024]{2,1,0:T(8,128)(2,1)S(1)}, bf16[2,256,1024]{2,1,0:T(8,128)(2,1)S(1)}, u32[]{:S(2)}, u32[]{:S(2)}) collective-permute-start(bf16[2,256,1024]{2,1,0:T(8,128)(2,1)S(1)} %get-tuple-element.23), channel_id=1, source_target_pairs={{0,4},{1,5},{2,6},{3,7},{4,8},{5,9},{6,10},{7,11},{8,12},{9,13},{1... | collective-permute-start | bytes 3145736 | tf_op jit(solution)/shard_map/ppermute | solution.py:31
  22.4 8.1 %collective-permute-start.6 = (bf16[2,256,1024]{2,1,0:T(8,128)(2,1)S(1)}, bf16[2,256,1024]{2,1,0:T(8,128)(2,1)S(1)}, u32[]{:S(2)}, u32[]{:S(2)}) collective-permute-start(bf16[2,256,1024]{2,1,0:T(8,128)(2,1)S(1)} %get-tuple-element.24), channel_id=1, source_target_pairs={{4,0},{5,1},{6,2},{7,3},{8,4},{9,5},{10,6},{11,7},{12,8},{13,9},{1... | collective-permute-start | bytes 3145736 | tf_op jit(solution)/shard_map/ppermute | solution.py:31
  30.5 2.0 %collective-permute-start.2 = (bf16[2,256,512]{2,1,0:T(8,128)(2,1)S(1)}, bf16[2,256,512]{2,1,0:T(8,128)(2,1)S(1)}, u32[]{:S(2)}, u32[]{:S(2)}) collective-permute-start(bf16[2,256,512]{2,1,0:T(8,128)(2,1)S(1)} %get-tuple-element.19), channel_id=1, source_target_pairs={{0,4},{1,5},{2,6},{3,7},{4,8},{5,9},{6,10},{7,11},{8,12},{9,13},{1... | collective-permute-start | bytes 1572872 | tf_op jit(solution)/shard_map/ppermute | solution.py:31
  32.5 80.6 %collective-permute-done.5.rest_2_ = bf16[2,256,1024]{2,1,0:T(8,128)(2,1)S(1)} collective-permute-done((bf16[2,256,1024]{2,1,0:T(8,128)(2,1)S(1)}, bf16[2,256,1024]{2,1,0:T(8,128)(2,1)S(1)}, u32[]{:S(2)}, u32[]{:S(2)}) %collective-permute-start.5) | collective-permute-done | bytes 1048608 | tf_op jit(solution)/shard_map/ppermute | solution.py:31
  113.1 1.9 %collective-permute-start.3 = (bf16[2,256,512]{2,1,0:T(8,128)(2,1)S(1)}, bf16[2,256,512]{2,1,0:T(8,128)(2,1)S(1)}, u32[]{:S(2)}, u32[]{:S(2)}) collective-permute-start(bf16[2,256,512]{2,1,0:T(8,128)(2,1)S(1)} %get-tuple-element.20), channel_id=1, source_target_pairs={{4,0},{5,1},{6,2},{7,3},{8,4},{9,5},{10,6},{11,7},{12,8},{13,9},{1... | collective-permute-start | bytes 1572872 | tf_op jit(solution)/shard_map/ppermute | solution.py:31
  115.1 1.2 warm_queries.1.table
  116.2 0.0 collective-permute-done.6.rest_3_
  116.2 0.0 collective-permute-done.1.rest_1_
  116.3 6.7 %shard_map.65 = (bf16[256,1024]{1,0:T(8,128)(2,1)S(1)}, bf16[256,1024]{1,0:T(8,128)(2,1)S(1)}) custom-call(s32[28]{0:T(128)S(1)} %warm_queries.1.table, bf16[512,1536]{1,0:T(8,128)(2,1)S(1)} %copy-done.2, bf16[512,1536]{1,0:T(8,128)(2,1)S(1)} %copy-done, bf16[512,1536]{1,0:T(8,128)(2,1)S(1)} %copy-done.1, ...), custom_call_target="tpu_custom_call" | custom-call | tf_op jit(solution)/shard_map/pallas_call | solution.py:295
  123.0 3.3 %collective-permute-start.7 = (bf16[256,1024]{1,0:T(8,128)(2,1)S(1)}, bf16[256,1024]{1,0:T(8,128)(2,1)S(1)}, u32[]{:S(2)}, u32[]{:S(2)}) collective-permute-start(bf16[256,1024]{1,0:T(8,128)(2,1)S(1)} %get-tuple-element.26), channel_id=1, source_target_pairs={{0,1},{1,0},{2,3},{3,2},{4,5},{5,4},{6,7},{7,6},{8,9},{9,8},{10,11... | collective-permute-start | bytes 1572872 | tf_op jit(solution)/shard_map/ppermute | solution.py:36
  126.3 0.0 collective-permute-done.2.rest_2_
  126.3 0.0 collective-permute-done.3.rest_3_
  126.3 3.7 %shard_map.64 = (bf16[256,512]{1,0:T(8,128)(2,1)S(1)}, bf16[256,512]{1,0:T(8,128)(2,1)S(1)}) custom-call(s32[28]{0:T(128)S(1)} %warm_queries.1.table, bf16[512,1536]{1,0:T(8,128)(2,1)S(1)} %copy-done.2, bf16[512,1536]{1,0:T(8,128)(2,1)S(1)} %copy-done, bf16[512,1536]{1,0:T(8,128)(2,1)S(1)} %copy-done.1, ...), custom_call_target="tpu_custom_call" | custom-call | tf_op jit(solution)/shard_map/pallas_call | solution.py:295
  130.0 4.1 %collective-permute-start.4 = (bf16[256,512]{1,0:T(8,128)(2,1)S(1)}, bf16[256,512]{1,0:T(8,128)(2,1)S(1)}, u32[]{:S(2)}, u32[]{:S(2)}) collective-permute-start(bf16[256,512]{1,0:T(8,128)(2,1)S(1)} %get-tuple-element.22), channel_id=1, source_target_pairs={{0,1},{1,0},{2,3},{3,2},{4,5},{5,4},{6,7},{7,6},{8,9},{9,8},{10,11... | collective-permute-start | bytes 786440 | tf_op jit(solution)/shard_map/ppermute | solution.py:36
  134.8 0.0 collective-permute-done.7.rest_1_
  134.8 1.1 shard_map.66.rest_2_
  135.9 0.0 collective-permute-done.4.rest_1_
  135.9 0.9 shard_map.67
  (11 shorter events, 0.0 us)
Async XLA Ops:
  0.0 11.1 %copy-start = (bf16[512,1536]{1,0:T(8,128)(2,1)S(1)}, bf16[512,1536]{1,0:T(8,128)(2,1)}, u32[]{:S(2)}) copy-start(bf16[512,1536]{1,0:T(8,128)(2,1)} %keys.7) | copy-start | bytes 4718596
  0.0 11.1 %copy-start.1 = (bf16[512,1536]{1,0:T(8,128)(2,1)S(1)}, bf16[512,1536]{1,0:T(8,128)(2,1)}, u32[]{:S(2)}) copy-start(bf16[512,1536]{1,0:T(8,128)(2,1)} %values.7) | copy-start | bytes 4718596
  0.0 11.1 %copy-start.4 = (s32[256,6]{0,1:T(8,128)S(1)}, s32[256,6]{0,1:T(8,128)}, u32[]{:S(2)}) copy-start(s32[256,6]{0,1:T(8,128)} %param.9) | copy-start | bytes 18436
  0.0 11.2 %copy-start.5 = (s32[256]{0:T(256)S(1)}, s32[256]{0:T(256)}, u32[]{:S(2)}) copy-start(s32[256]{0:T(256)} %counts.3) | copy-start | bytes 3076
  4.6 111.7 %collective-permute-start.1 = (bf16[2,256,1536]{2,1,0:T(8,128)(2,1)}, bf16[2,256,1536]{2,1,0:T(8,128)(2,1)S(1)}, u32[]{:S(2)}, u32[]{:S(2)}) collective-permute-start(bf16[2,256,1536]{2,1,0:T(8,128)(2,1)} %get-tuple-element.18), channel_id=1, source_target_pairs={{2,0},{3,1},{4,2},{5,3},{6,4},{7,5},{8,6},{9,7},{10,8},{11,9},{12,... | collective-permute-start | bytes 4718600 | tf_op jit(solution)/shard_map/ppermute | solution.py:31
  6.5 108.5 %copy-start.2 = (bf16[512,1536]{1,0:T(8,128)(2,1)S(1)}, bf16[512,1536]{1,0:T(8,128)(2,1)}, u32[]{:S(2)}) copy-start(bf16[512,1536]{1,0:T(8,128)(2,1)} %queries.5) | copy-start | bytes 4718596
  6.6 109.7 %collective-permute-start = (bf16[2,256,1536]{2,1,0:T(8,128)(2,1)}, bf16[2,256,1536]{2,1,0:T(8,128)(2,1)S(1)}, u32[]{:S(2)}, u32[]{:S(2)}) collective-permute-start(bf16[2,256,1536]{2,1,0:T(8,128)(2,1)} %get-tuple-element.16.near), channel_id=1, source_target_pairs={{0,2},{1,3},{2,4},{3,5},{4,6},{5,7},{6,8},{7,9},{8,10},{9,11},{10,... | collective-permute-start | bytes 4718600 | tf_op jit(solution)/shard_map/ppermute | solution.py:31
  11.2 1.4 %copy-start.3 = (bf16[2,256,1536]{2,1,0:T(8,128)(2,1)S(1)}, bf16[2,256,1536]{2,1,0:T(8,128)(2,1)}, u32[]{:S(2)}) copy-start(bf16[2,256,1536]{2,1,0:T(8,128)(2,1)} %get-tuple-element.16.near) | copy-start | bytes 4718596
  14.6 98.6 %collective-permute-start.5 = (bf16[2,256,1024]{2,1,0:T(8,128)(2,1)S(1)}, bf16[2,256,1024]{2,1,0:T(8,128)(2,1)S(1)}, u32[]{:S(2)}, u32[]{:S(2)}) collective-permute-start(bf16[2,256,1024]{2,1,0:T(8,128)(2,1)S(1)} %get-tuple-element.23), channel_id=1, source_target_pairs={{0,4},{1,5},{2,6},{3,7},{4,8},{5,9},{6,10},{7,11},{8,12},{9,13},{1... | collective-permute-start | bytes 3145736 | tf_op jit(solution)/shard_map/ppermute | solution.py:31
  22.4 93.8 %collective-permute-start.6 = (bf16[2,256,1024]{2,1,0:T(8,128)(2,1)S(1)}, bf16[2,256,1024]{2,1,0:T(8,128)(2,1)S(1)}, u32[]{:S(2)}, u32[]{:S(2)}) collective-permute-start(bf16[2,256,1024]{2,1,0:T(8,128)(2,1)S(1)} %get-tuple-element.24), channel_id=1, source_target_pairs={{4,0},{5,1},{6,2},{7,3},{8,4},{9,5},{10,6},{11,7},{12,8},{13,9},{1... | collective-permute-start | bytes 3145736 | tf_op jit(solution)/shard_map/ppermute | solution.py:31
  30.5 95.7 %collective-permute-start.2 = (bf16[2,256,512]{2,1,0:T(8,128)(2,1)S(1)}, bf16[2,256,512]{2,1,0:T(8,128)(2,1)S(1)}, u32[]{:S(2)}, u32[]{:S(2)}) collective-permute-start(bf16[2,256,512]{2,1,0:T(8,128)(2,1)S(1)} %get-tuple-element.19), channel_id=1, source_target_pairs={{0,4},{1,5},{2,6},{3,7},{4,8},{5,9},{6,10},{7,11},{8,12},{9,13},{1... | collective-permute-start | bytes 1572872 | tf_op jit(solution)/shard_map/ppermute | solution.py:31
  113.1 13.2 %collective-permute-start.3 = (bf16[2,256,512]{2,1,0:T(8,128)(2,1)S(1)}, bf16[2,256,512]{2,1,0:T(8,128)(2,1)S(1)}, u32[]{:S(2)}, u32[]{:S(2)}) collective-permute-start(bf16[2,256,512]{2,1,0:T(8,128)(2,1)S(1)} %get-tuple-element.20), channel_id=1, source_target_pairs={{4,0},{5,1},{6,2},{7,3},{8,4},{9,5},{10,6},{11,7},{12,8},{13,9},{1... | collective-permute-start | bytes 1572872 | tf_op jit(solution)/shard_map/ppermute | solution.py:31
  123.0 11.8 %collective-permute-start.7 = (bf16[256,1024]{1,0:T(8,128)(2,1)S(1)}, bf16[256,1024]{1,0:T(8,128)(2,1)S(1)}, u32[]{:S(2)}, u32[]{:S(2)}) collective-permute-start(bf16[256,1024]{1,0:T(8,128)(2,1)S(1)} %get-tuple-element.26), channel_id=1, source_target_pairs={{0,1},{1,0},{2,3},{3,2},{4,5},{5,4},{6,7},{7,6},{8,9},{9,8},{10,11... | collective-permute-start | bytes 1572872 | tf_op jit(solution)/shard_map/ppermute | solution.py:36
  130.0 5.9 %collective-permute-start.4 = (bf16[256,512]{1,0:T(8,128)(2,1)S(1)}, bf16[256,512]{1,0:T(8,128)(2,1)S(1)}, u32[]{:S(2)}, u32[]{:S(2)}) collective-permute-start(bf16[256,512]{1,0:T(8,128)(2,1)S(1)} %get-tuple-element.22), channel_id=1, source_target_pairs={{0,1},{1,0},{2,3},{3,2},{4,5},{5,4},{6,7},{7,6},{8,9},{9,8},{10,11... | collective-permute-start | bytes 786440 | tf_op jit(solution)/shard_map/ppermute | solution.py:36
